TPU v7x, 32 devices: a whole 2x2x4 slice. The times are simulated.
32 devices in a mesh: image: 4 (over y, x), space: 8 (over z, core).
Axes of the slice: x: 2, y: 2, z: 4, core: 2. Of those that a mesh axis runs over, the one named last changes fastest.
Arguments:
- positions: float32 [4, 3, 8192], P('image', None, 'space'), may hold values from -20 to 20
- neighbours: int32 [64, 3], replicated, may hold values from 0 to 4
- brackets: int32 [4], P('image'), may hold values from 0 to 2, as said below
- codes: int32 [4], P('image'), may hold values from 0 to 65535
Outputs:
- new_images: float32 [4, 3, 8192], P('image', None, 'space')
- arc_fraction: float32 [4], P('image')
Inputs may be any that keep to these rules, and one draw needn't show every extreme that they name: brackets[j] lies between j - 1 and j + 1 - 1; both ends of that window are reached.
All inputs are finite; a program needn't handle non-finite values.
Results may differ from a plain program's by a relative error of at most 0.0003.
Values sent between devices are 32-bit elements; how exact they have to be, the bound alone decides.
No kernel may reach another device: no remote copies, remote signals or barrier semaphores. Data moves between devices by JAX's collectives and lax.ppermute only.
A program may use at most 64 MiB of HBM per device.

v0:
```python
import jax
import jax.numpy as jnp
from jax import lax
from jax.sharding import PartitionSpec as P

PROT_DEV = 128
BLOCK = 128
HALO = 2
STEPS = 10


TIME_STEP = 0.05
RESTRAINT = 1.0
COUPLING = 3.0
KERNEL_RATE = 0.125
EPSILON = 1e-06
CODE_SCALE = 65536.0


def extended(cells, sides, width, closed):
    for axis, dim in sides:
        count = lax.axis_size(axis)
        ends = count if closed else count - 1
        head = lax.slice_in_dim(cells, 0, width, axis=dim)
        tail = lax.slice_in_dim(cells, cells.shape[dim] - width, cells.shape[dim], axis=dim)
        cells = jnp.concatenate(
            [
                lax.ppermute(tail, axis, [(i, (i + 1) % count) for i in range(ends)]),
                cells,
                lax.ppermute(head, axis, [((i + 1) % count, i) for i in range(ends)]),
            ],
            axis=dim,
        )
    return cells


def passed_along(block, axis, distance):
    devices = range(lax.axis_size(axis))
    route = [(i - distance, i) for i in devices if i - distance in devices]
    return lax.ppermute(block, axis, route)


def carried_in(value, axis, join, neutral):
    count, mine = (lax.axis_size(axis), lax.axis_index(axis))
    pieces = lax.all_gather(value, axis)
    so_far = jnp.full_like(value, 0) + jnp.asarray(neutral, value.dtype)

    def step(position, so_far):
        longer = join(so_far, pieces[position])
        return jnp.where(position < mine, longer, so_far)

    return lax.fori_loop(0, count - 1, step, so_far)


def pair_forces(swarm_centres, partner_beads):
    centre_sq = jnp.sum(swarm_centres * swarm_centres, axis=-3)
    partner_sq = jnp.sum(partner_beads * partner_beads, axis=-3)
    crossing_flags = jnp.einsum(
        "...euh,...euw->...uhw", swarm_centres, partner_beads, precision=lax.Precision.HIGHEST
    )
    weight_factors = jnp.exp(
        -KERNEL_RATE * (centre_sq[..., :, None] + partner_sq[..., None, :] - 2.0 * crossing_flags)
    )
    row_sums = jnp.sum(weight_factors, axis=-1)
    pulled_images = jnp.einsum(
        "...aun,...san->...sau", weight_factors, partner_beads, precision=lax.Precision.HIGHEST
    )
    return (
        COUPLING
        / partner_beads.shape[-1]
        * (swarm_centres * row_sums[..., None, :, :] - pulled_images)
    )


def block_forces(widened, offset_table, centre_count):
    block_beads = widened.shape[3]
    partner_count = offset_table.shape[1]
    partner_rows = jnp.arange(centre_count, dtype=jnp.int32)[:, None] + offset_table
    centres = widened[..., HALO : HALO + centre_count, :]
    partners = jnp.take(widened, partner_rows, axis=-2)
    lead = partners.shape[:-3]
    partners = partners.reshape(lead + (centre_count, partner_count * block_beads))
    return pair_forces(centres, partners)


def add_lengths(earlier, later):
    return earlier + later


def body(positions, neighbours, brackets, codes):
    per_device = positions.shape[0]
    slab_beads = positions.shape[2]
    blocks_own = slab_beads // BLOCK
    slab_id = lax.axis_index("space")
    total_blocks = lax.axis_size("space") * blocks_own
    bead_index = jnp.arange(slab_beads, dtype=jnp.int32).reshape(blocks_own, BLOCK)
    restrain = (bead_index < PROT_DEV).astype(jnp.float32)
    anchor = positions.reshape(per_device, 3, blocks_own, BLOCK)
    own_table = lax.dynamic_slice_in_dim(neighbours, slab_id * blocks_own, blocks_own, 0)
    widened_count = blocks_own + 4 * HALO
    middle = blocks_own + 2 * HALO

    def deep_rims(state_now):
        padded = extended(state_now, (("space", 2),), 2 * HALO * BLOCK, True)
        return padded.reshape(per_device, 3, widened_count, BLOCK)

    row_ids = (slab_id * blocks_own - HALO + jnp.arange(middle, dtype=jnp.int32)) % total_blocks
    middle_table = jnp.take(neighbours, row_ids, axis=0)
    wide_blocks = (jnp.arange(widened_count, dtype=jnp.int32) - 2 * HALO) % blocks_own
    wide_beads = wide_blocks[:, None] * BLOCK + jnp.arange(BLOCK, dtype=jnp.int32)[None, :]
    middle_restrain = (wide_beads[HALO : HALO + middle] < PROT_DEV).astype(jnp.float32)
    middle_anchor = deep_rims(positions)[:, :, HALO : HALO + middle]

    def advance_pair(turn_index, current):
        widened = deep_rims(current)
        centre = widened[:, :, HALO : HALO + middle]
        forces = block_forces(widened, middle_table, middle)
        stepped = centre + TIME_STEP * (
            forces - RESTRAINT * middle_restrain * (centre - middle_anchor)
        )
        owned = stepped[:, :, HALO : HALO + blocks_own]
        forces = block_forces(stepped, own_table, blocks_own)
        advanced = owned + TIME_STEP * (forces - RESTRAINT * restrain * (owned - anchor))
        return advanced.reshape(per_device, 3, slab_beads)

    evolved = lax.fori_loop(0, STEPS // 2, advance_pair, positions)
    protein = evolved[:, :, :PROT_DEV]
    before = passed_along(protein[per_device - 1], "image", 1)
    earlier = jnp.concatenate([before[None], protein[: per_device - 1]], axis=0)
    differences = protein - earlier
    partial_value = jnp.sum(differences * differences, axis=(1, 2))
    squares = lax.psum(partial_value, "space")
    image_count = lax.axis_size("image") * per_device
    first_id = lax.axis_index("image") * per_device
    global_ids = first_id + jnp.arange(per_device, dtype=jnp.int32)
    step_length = jnp.where(global_ids > 0, jnp.sqrt(squares + EPSILON), 0.0)
    running = jnp.cumsum(step_length)
    offset = carried_in(running[per_device - 1], "image", add_lengths, jnp.zeros((), jnp.float32))
    length_total = lax.psum(running[per_device - 1], "image")
    arc_here = offset + running
    old_images = extended(evolved, (("image", 0),), per_device, False)
    arc_values = extended(arc_here, (("image", 0),), per_device, False)
    root = first_id - per_device
    local_index = brackets - root
    places = jnp.arange(old_images.shape[0], dtype=jnp.int32)
    lower_pick = (places[None, :] == local_index[:, None]).astype(jnp.float32)
    upper_pick = (places[None, :] == local_index[:, None] + 1).astype(jnp.float32)
    arc_lower = jnp.sum(lower_pick * arc_values[None, :], axis=1)
    upper_arc_bound = jnp.sum(upper_pick * arc_values[None, :], axis=1)
    target = (brackets.astype(jnp.float32) + codes.astype(jnp.float32) / CODE_SCALE) / (
        image_count - 1
    )
    weight = (target * length_total - arc_lower) / (upper_arc_bound - arc_lower)
    mixing = (1.0 - weight)[:, None] * lower_pick + weight[:, None] * upper_pick
    new_images = jnp.einsum("ie,ecb->icb", mixing, old_images, precision=lax.Precision.HIGHEST)
    return (new_images, arc_here / length_total)


def solution(mesh):
    placed = (P("image", None, "space"), P(), P("image"), P("image"))
    return jax.shard_map(
        body,
        mesh=mesh,
        in_specs=placed,
        out_specs=(P("image", None, "space"), P("image")),
        check_vma=False,
    )
```

profile of v0, /device:TPU:4, one launch (start us, length us, event | category | flops | bytes accessed | tf_op | source)
XLA Modules:
  0.0 153.7 jit_solution(15413815239639958526)
XLA Ops:
  0.6 0.7 fusion.57
  1.3 3.5 %collective-permute-start.3 = (f32[1,3,512]{2,0,1:T(1,128)S(1)}, f32[1,3,512]{2,0,1:T(1,128)S(1)}, u32[]{:S(2)}, u32[]{:S(2)}) collective-permute-start(f32[1,3,512]{2,0,1:T(1,128)S(1)} %get-tuple-element.209), channel_id=1, source_target_pairs={{1,0},{2,1},{3,2},{4,3},{5,4},{6,5},{7,6},{0,7},{9,8},{10,9},{11,1... | collective-permute-start | bytes 18440 | tf_op jit(solution)/shard_map/ppermute | solution.py:30
  5.0 0.8 copy.54
  5.9 0.6 gather_fusion.2
  6.5 0.8 constant_dynamic-slice_fusion
  7.3 0.7 copy.55
  8.1 0.7 copy.58
  8.8 0.7 pad_maximum_fusion.1
  9.6 82.7 %while.25 = (s32[]{:T(128)}, f32[1,3,1024]{2,1,0:T(4,128)S(1)}, s32[12,3]{0,1:T(4,128)S(1)}, f32[12,128]{1,0:T(8,128)S(1)}, f32[1,3,12,128]{3,1,2,0:T(4,128)S(1)...) while((s32[]{:T(128)}, f32[1,3,1024]{2,1,0:T(4,128)S(1)}, ...), condition=%wide.region_7.8_spmd.clone, body=%wide.region_0.7_spmd.clone.sunk | while | flops 75880080 | bytes 8957014 | solution.py:126
  9.7 3.5 %collective-permute-start.1 = (f32[1,3,512]{2,1,0:T(4,128)S(1)}, f32[1,3,512]{2,1,0:T(4,128)S(1)}, u32[]{:S(2)}, u32[]{:S(2)}) collective-permute-start(f32[1,3,512]{2,1,0:T(4,128)S(1)} %get-tuple-element.285), channel_id=1, source_target_pairs={{1,0},{2,1},{3,2},{4,3},{5,4},{6,5},{7,6},{0,7},{9,8},{10,9},{11,1... | collective-permute-start | bytes 18440 | tf_op jit(solution)/shard_map/while/body/eval_jaxpr/ppermute | solution.py:30
  14.0 0.5 collective-permute-done
  14.6 0.6 gather_fusion
  15.4 3.3 %fusion.74 = (f32[12,128]{1,0:T(8,128)S(1)}, f32[12,128,384]{2,1,0:T(8,128)S(1)}) fusion(f32[3,12,384]{2,0,1:T(4,128)S(1)} %bitcast.159, pred[12,384]{1,0:T(8,128)(4,1)S(1)} %bitcast.173, f32[1,3,16,128]{3,1,2,0:T(4,128)S(1)} %bitcast.163, f32[12,384]{1,0:T(8,128)S(1)} %bitcast.172, f32[12,128]{1,0:T(8,128)S(1)} %multiply_reduce_fusion.9), kind=kOutput, calls=%fused_computation.106.clone.1 | convolution fusion | flops 24195072 | bytes 2502656 | tf_op jit(solution)/shard_map/while/body/eval_jaxpr/...euh,...euw->...uhw/dot_general | solution.py:58
  18.7 2.6 %multiply_add_fusion.2 = f32[1,3,12,128]{3,1,2,0:T(4,128)S(1)} fusion(f32[1,3,12,128]{3,1,2,0:T(4,128)S(1)} %get-tuple-element.314, f32[1,3,16,128]{3,1,2,0:T(4,128)S(1)} %bitcast.164, f32[12,128]{1,0:T(8,128)S(1)} %get-tuple-element.313, f32[12,128]{1,0:T(8,128)S(1)} %get-tuple-element.286, f32[12,128,384]{2,1,0:T(8,128)S(1)} %get-tuple-element.287, ...), kind=kOutput, calls=%fused_computation.27.clone.1 | convolution fusion | flops 21284352 | bytes 2486784 | tf_op jit(solution)/shard_map/while/body/eval_jaxpr/...aun,...san->...sau/dot_general | solution.py:65
  21.3 0.6 gather_fusion.1
  22.0 2.3 %fusion.75 = (f32[8,128]{1,0:T(8,128)S(1)}, f32[8,128,384]{2,1,0:T(8,128)S(1)}) fusion(f32[3,8,384]{2,0,1:T(4,128)S(1)} %bitcast.167, pred[8,384]{1,0:T(8,128)(4,1)S(1)} %broadcast_bitcast_fusion.2, f32[1,3,12,128]{3,1,2,0:T(4,128)S(1)} %multiply_add_fusion.2, f32[8,384]{1,0:T(8,128)S(1)} %bitcast.175, f32[8,128]{1,0:T(8,128)S(1)} %multiply_reduce_fusion.11), kind=kOutput, calls=%fused_computation.107.clone.1 | convolution fusion | flops 16130048 | bytes 1661952 | tf_op jit(solution)/shard_map/while/body/eval_jaxpr/...euh,...euw->...uhw/dot_general | solution.py:58
  24.3 1.8 %fusion.77 = f32[1,3,1024]{2,1,0:T(4,128)S(1)} fusion(f32[8,128,384]{2,1,0:T(8,128)S(1)} %get-tuple-element.288, f32[3,8,384]{2,0,1:T(4,128)S(1)} %bitcast.168, pred[8,384]{1,0:T(8,128)(4,1)S(1)} %broadcast_bitcast_fusion.2, f32[1,3,8,128]{3,1,2,0:T(4,128)S(1)} %get-tuple-element.316, f32[1,3,12,128]{3,1,2,0:T(4,128)S(1)} %multiply_add_fusion.2, ...), kind=kOutput, calls=%fused_computation.13.clone.1 | convolution fusion | flops 14189568 | bytes 1657856 | tf_op jit(solution)/shard_map/while/body/eval_jaxpr/...aun,...san->...sau/dot_general | solution.py:65
  26.2 3.6 %collective-permute-start.1 = (f32[1,3,512]{2,1,0:T(4,128)S(1)}, f32[1,3,512]{2,1,0:T(4,128)S(1)}, u32[]{:S(2)}, u32[]{:S(2)}) collective-permute-start(f32[1,3,512]{2,1,0:T(4,128)S(1)} %get-tuple-element.285), channel_id=1, source_target_pairs={{1,0},{2,1},{3,2},{4,3},{5,4},{6,5},{7,6},{0,7},{9,8},{10,9},{11,1... | collective-permute-start | bytes 18440 | tf_op jit(solution)/shard_map/while/body/eval_jaxpr/ppermute | solution.py:30
  30.6 0.5 collective-permute-done
  31.1 0.6 gather_fusion
  31.9 3.3 %fusion.74 = (f32[12,128]{1,0:T(8,128)S(1)}, f32[12,128,384]{2,1,0:T(8,128)S(1)}) fusion(f32[3,12,384]{2,0,1:T(4,128)S(1)} %bitcast.159, pred[12,384]{1,0:T(8,128)(4,1)S(1)} %bitcast.173, f32[1,3,16,128]{3,1,2,0:T(4,128)S(1)} %bitcast.163, f32[12,384]{1,0:T(8,128)S(1)} %bitcast.172, f32[12,128]{1,0:T(8,128)S(1)} %multiply_reduce_fusion.9), kind=kOutput, calls=%fused_computation.106.clone.1 | convolution fusion | flops 24195072 | bytes 2502656 | tf_op jit(solution)/shard_map/while/body/eval_jaxpr/...euh,...euw->...uhw/dot_general | solution.py:58
  35.2 2.6 %multiply_add_fusion.2 = f32[1,3,12,128]{3,1,2,0:T(4,128)S(1)} fusion(f32[1,3,12,128]{3,1,2,0:T(4,128)S(1)} %get-tuple-element.314, f32[1,3,16,128]{3,1,2,0:T(4,128)S(1)} %bitcast.164, f32[12,128]{1,0:T(8,128)S(1)} %get-tuple-element.313, f32[12,128]{1,0:T(8,128)S(1)} %get-tuple-element.286, f32[12,128,384]{2,1,0:T(8,128)S(1)} %get-tuple-element.287, ...), kind=kOutput, calls=%fused_computation.27.clone.1 | convolution fusion | flops 21284352 | bytes 2486784 | tf_op jit(solution)/shard_map/while/body/eval_jaxpr/...aun,...san->...sau/dot_general | solution.py:65
  37.8 0.6 gather_fusion.1
  38.6 2.3 %fusion.75 = (f32[8,128]{1,0:T(8,128)S(1)}, f32[8,128,384]{2,1,0:T(8,128)S(1)}) fusion(f32[3,8,384]{2,0,1:T(4,128)S(1)} %bitcast.167, pred[8,384]{1,0:T(8,128)(4,1)S(1)} %broadcast_bitcast_fusion.2, f32[1,3,12,128]{3,1,2,0:T(4,128)S(1)} %multiply_add_fusion.2, f32[8,384]{1,0:T(8,128)S(1)} %bitcast.175, f32[8,128]{1,0:T(8,128)S(1)} %multiply_reduce_fusion.11), kind=kOutput, calls=%fused_computation.107.clone.1 | convolution fusion | flops 16130048 | bytes 1661952 | tf_op jit(solution)/shard_map/while/body/eval_jaxpr/...euh,...euw->...uhw/dot_general | solution.py:58
  40.8 1.8 %fusion.77 = f32[1,3,1024]{2,1,0:T(4,128)S(1)} fusion(f32[8,128,384]{2,1,0:T(8,128)S(1)} %get-tuple-element.288, f32[3,8,384]{2,0,1:T(4,128)S(1)} %bitcast.168, pred[8,384]{1,0:T(8,128)(4,1)S(1)} %broadcast_bitcast_fusion.2, f32[1,3,8,128]{3,1,2,0:T(4,128)S(1)} %get-tuple-element.316, f32[1,3,12,128]{3,1,2,0:T(4,128)S(1)} %multiply_add_fusion.2, ...), kind=kOutput, calls=%fused_computation.13.clone.1 | convolution fusion | flops 14189568 | bytes 1657856 | tf_op jit(solution)/shard_map/while/body/eval_jaxpr/...aun,...san->...sau/dot_general | solution.py:65
  42.7 3.6 %collective-permute-start.1 = (f32[1,3,512]{2,1,0:T(4,128)S(1)}, f32[1,3,512]{2,1,0:T(4,128)S(1)}, u32[]{:S(2)}, u32[]{:S(2)}) collective-permute-start(f32[1,3,512]{2,1,0:T(4,128)S(1)} %get-tuple-element.285), channel_id=1, source_target_pairs={{1,0},{2,1},{3,2},{4,3},{5,4},{6,5},{7,6},{0,7},{9,8},{10,9},{11,1... | collective-permute-start | bytes 18440 | tf_op jit(solution)/shard_map/while/body/eval_jaxpr/ppermute | solution.py:30
  47.1 0.5 collective-permute-done
  47.6 0.6 gather_fusion
  48.5 3.3 %fusion.74 = (f32[12,128]{1,0:T(8,128)S(1)}, f32[12,128,384]{2,1,0:T(8,128)S(1)}) fusion(f32[3,12,384]{2,0,1:T(4,128)S(1)} %bitcast.159, pred[12,384]{1,0:T(8,128)(4,1)S(1)} %bitcast.173, f32[1,3,16,128]{3,1,2,0:T(4,128)S(1)} %bitcast.163, f32[12,384]{1,0:T(8,128)S(1)} %bitcast.172, f32[12,128]{1,0:T(8,128)S(1)} %multiply_reduce_fusion.9), kind=kOutput, calls=%fused_computation.106.clone.1 | convolution fusion | flops 24195072 | bytes 2502656 | tf_op jit(solution)/shard_map/while/body/eval_jaxpr/...euh,...euw->...uhw/dot_general | solution.py:58
  51.7 2.6 %multiply_add_fusion.2 = f32[1,3,12,128]{3,1,2,0:T(4,128)S(1)} fusion(f32[1,3,12,128]{3,1,2,0:T(4,128)S(1)} %get-tuple-element.314, f32[1,3,16,128]{3,1,2,0:T(4,128)S(1)} %bitcast.164, f32[12,128]{1,0:T(8,128)S(1)} %get-tuple-element.313, f32[12,128]{1,0:T(8,128)S(1)} %get-tuple-element.286, f32[12,128,384]{2,1,0:T(8,128)S(1)} %get-tuple-element.287, ...), kind=kOutput, calls=%fused_computation.27.clone.1 | convolution fusion | flops 21284352 | bytes 2486784 | tf_op jit(solution)/shard_map/while/body/eval_jaxpr/...aun,...san->...sau/dot_general | solution.py:65
  54.4 0.6 gather_fusion.1
  55.1 2.3 %fusion.75 = (f32[8,128]{1,0:T(8,128)S(1)}, f32[8,128,384]{2,1,0:T(8,128)S(1)}) fusion(f32[3,8,384]{2,0,1:T(4,128)S(1)} %bitcast.167, pred[8,384]{1,0:T(8,128)(4,1)S(1)} %broadcast_bitcast_fusion.2, f32[1,3,12,128]{3,1,2,0:T(4,128)S(1)} %multiply_add_fusion.2, f32[8,384]{1,0:T(8,128)S(1)} %bitcast.175, f32[8,128]{1,0:T(8,128)S(1)} %multiply_reduce_fusion.11), kind=kOutput, calls=%fused_computation.107.clone.1 | convolution fusion | flops 16130048 | bytes 1661952 | tf_op jit(solution)/shard_map/while/body/eval_jaxpr/...euh,...euw->...uhw/dot_general | solution.py:58
  57.4 1.8 %fusion.77 = f32[1,3,1024]{2,1,0:T(4,128)S(1)} fusion(f32[8,128,384]{2,1,0:T(8,128)S(1)} %get-tuple-element.288, f32[3,8,384]{2,0,1:T(4,128)S(1)} %bitcast.168, pred[8,384]{1,0:T(8,128)(4,1)S(1)} %broadcast_bitcast_fusion.2, f32[1,3,8,128]{3,1,2,0:T(4,128)S(1)} %get-tuple-element.316, f32[1,3,12,128]{3,1,2,0:T(4,128)S(1)} %multiply_add_fusion.2, ...), kind=kOutput, calls=%fused_computation.13.clone.1 | convolution fusion | flops 14189568 | bytes 1657856 | tf_op jit(solution)/shard_map/while/body/eval_jaxpr/...aun,...san->...sau/dot_general | solution.py:65
  59.2 3.6 %collective-permute-start.1 = (f32[1,3,512]{2,1,0:T(4,128)S(1)}, f32[1,3,512]{2,1,0:T(4,128)S(1)}, u32[]{:S(2)}, u32[]{:S(2)}) collective-permute-start(f32[1,3,512]{2,1,0:T(4,128)S(1)} %get-tuple-element.285), channel_id=1, source_target_pairs={{1,0},{2,1},{3,2},{4,3},{5,4},{6,5},{7,6},{0,7},{9,8},{10,9},{11,1... | collective-permute-start | bytes 18440 | tf_op jit(solution)/shard_map/while/body/eval_jaxpr/ppermute | solution.py:30
  63.6 0.5 collective-permute-done
  64.2 0.6 gather_fusion
  65.0 3.3 %fusion.74 = (f32[12,128]{1,0:T(8,128)S(1)}, f32[12,128,384]{2,1,0:T(8,128)S(1)}) fusion(f32[3,12,384]{2,0,1:T(4,128)S(1)} %bitcast.159, pred[12,384]{1,0:T(8,128)(4,1)S(1)} %bitcast.173, f32[1,3,16,128]{3,1,2,0:T(4,128)S(1)} %bitcast.163, f32[12,384]{1,0:T(8,128)S(1)} %bitcast.172, f32[12,128]{1,0:T(8,128)S(1)} %multiply_reduce_fusion.9), kind=kOutput, calls=%fused_computation.106.clone.1 | convolution fusion | flops 24195072 | bytes 2502656 | tf_op jit(solution)/shard_map/while/body/eval_jaxpr/...euh,...euw->...uhw/dot_general | solution.py:58
  68.3 2.6 %multiply_add_fusion.2 = f32[1,3,12,128]{3,1,2,0:T(4,128)S(1)} fusion(f32[1,3,12,128]{3,1,2,0:T(4,128)S(1)} %get-tuple-element.314, f32[1,3,16,128]{3,1,2,0:T(4,128)S(1)} %bitcast.164, f32[12,128]{1,0:T(8,128)S(1)} %get-tuple-element.313, f32[12,128]{1,0:T(8,128)S(1)} %get-tuple-element.286, f32[12,128,384]{2,1,0:T(8,128)S(1)} %get-tuple-element.287, ...), kind=kOutput, calls=%fused_computation.27.clone.1 | convolution fusion | flops 21284352 | bytes 2486784 | tf_op jit(solution)/shard_map/while/body/eval_jaxpr/...aun,...san->...sau/dot_general | solution.py:65
  70.9 0.6 gather_fusion.1
  71.7 2.3 %fusion.75 = (f32[8,128]{1,0:T(8,128)S(1)}, f32[8,128,384]{2,1,0:T(8,128)S(1)}) fusion(f32[3,8,384]{2,0,1:T(4,128)S(1)} %bitcast.167, pred[8,384]{1,0:T(8,128)(4,1)S(1)} %broadcast_bitcast_fusion.2, f32[1,3,12,128]{3,1,2,0:T(4,128)S(1)} %multiply_add_fusion.2, f32[8,384]{1,0:T(8,128)S(1)} %bitcast.175, f32[8,128]{1,0:T(8,128)S(1)} %multiply_reduce_fusion.11), kind=kOutput, calls=%fused_computation.107.clone.1 | convolution fusion | flops 16130048 | bytes 1661952 | tf_op jit(solution)/shard_map/while/body/eval_jaxpr/...euh,...euw->...uhw/dot_general | solution.py:58
  73.9 1.8 %fusion.77 = f32[1,3,1024]{2,1,0:T(4,128)S(1)} fusion(f32[8,128,384]{2,1,0:T(8,128)S(1)} %get-tuple-element.288, f32[3,8,384]{2,0,1:T(4,128)S(1)} %bitcast.168, pred[8,384]{1,0:T(8,128)(4,1)S(1)} %broadcast_bitcast_fusion.2, f32[1,3,8,128]{3,1,2,0:T(4,128)S(1)} %get-tuple-element.316, f32[1,3,12,128]{3,1,2,0:T(4,128)S(1)} %multiply_add_fusion.2, ...), kind=kOutput, calls=%fused_computation.13.clone.1 | convolution fusion | flops 14189568 | bytes 1657856 | tf_op jit(solution)/shard_map/while/body/eval_jaxpr/...aun,...san->...sau/dot_general | solution.py:65
  75.8 3.6 %collective-permute-start.1 = (f32[1,3,512]{2,1,0:T(4,128)S(1)}, f32[1,3,512]{2,1,0:T(4,128)S(1)}, u32[]{:S(2)}, u32[]{:S(2)}) collective-permute-start(f32[1,3,512]{2,1,0:T(4,128)S(1)} %get-tuple-element.285), channel_id=1, source_target_pairs={{1,0},{2,1},{3,2},{4,3},{5,4},{6,5},{7,6},{0,7},{9,8},{10,9},{11,1... | collective-permute-start | bytes 18440 | tf_op jit(solution)/shard_map/while/body/eval_jaxpr/ppermute | solution.py:30
  80.7 0.6 gather_fusion
  81.5 3.3 %fusion.74 = (f32[12,128]{1,0:T(8,128)S(1)}, f32[12,128,384]{2,1,0:T(8,128)S(1)}) fusion(f32[3,12,384]{2,0,1:T(4,128)S(1)} %bitcast.159, pred[12,384]{1,0:T(8,128)(4,1)S(1)} %bitcast.173, f32[1,3,16,128]{3,1,2,0:T(4,128)S(1)} %bitcast.163, f32[12,384]{1,0:T(8,128)S(1)} %bitcast.172, f32[12,128]{1,0:T(8,128)S(1)} %multiply_reduce_fusion.9), kind=kOutput, calls=%fused_computation.106.clone.1 | convolution fusion | flops 24195072 | bytes 2502656 | tf_op jit(solution)/shard_map/while/body/eval_jaxpr/...euh,...euw->...uhw/dot_general | solution.py:58
  84.8 2.6 %multiply_add_fusion.2 = f32[1,3,12,128]{3,1,2,0:T(4,128)S(1)} fusion(f32[1,3,12,128]{3,1,2,0:T(4,128)S(1)} %get-tuple-element.314, f32[1,3,16,128]{3,1,2,0:T(4,128)S(1)} %bitcast.164, f32[12,128]{1,0:T(8,128)S(1)} %get-tuple-element.313, f32[12,128]{1,0:T(8,128)S(1)} %get-tuple-element.286, f32[12,128,384]{2,1,0:T(8,128)S(1)} %get-tuple-element.287, ...), kind=kOutput, calls=%fused_computation.27.clone.1 | convolution fusion | flops 21284352 | bytes 2486784 | tf_op jit(solution)/shard_map/while/body/eval_jaxpr/...aun,...san->...sau/dot_general | solution.py:65
  87.5 0.6 gather_fusion.1
  88.2 2.3 %fusion.75 = (f32[8,128]{1,0:T(8,128)S(1)}, f32[8,128,384]{2,1,0:T(8,128)S(1)}) fusion(f32[3,8,384]{2,0,1:T(4,128)S(1)} %bitcast.167, pred[8,384]{1,0:T(8,128)(4,1)S(1)} %broadcast_bitcast_fusion.2, f32[1,3,12,128]{3,1,2,0:T(4,128)S(1)} %multiply_add_fusion.2, f32[8,384]{1,0:T(8,128)S(1)} %bitcast.175, f32[8,128]{1,0:T(8,128)S(1)} %multiply_reduce_fusion.11), kind=kOutput, calls=%fused_computation.107.clone.1 | convolution fusion | flops 16130048 | bytes 1661952 | tf_op jit(solution)/shard_map/while/body/eval_jaxpr/...euh,...euw->...uhw/dot_general | solution.py:58
  90.5 1.8 %fusion.77 = f32[1,3,1024]{2,1,0:T(4,128)S(1)} fusion(f32[8,128,384]{2,1,0:T(8,128)S(1)} %get-tuple-element.288, f32[3,8,384]{2,0,1:T(4,128)S(1)} %bitcast.168, pred[8,384]{1,0:T(8,128)(4,1)S(1)} %broadcast_bitcast_fusion.2, f32[1,3,8,128]{3,1,2,0:T(4,128)S(1)} %get-tuple-element.316, f32[1,3,12,128]{3,1,2,0:T(4,128)S(1)} %multiply_add_fusion.2, ...), kind=kOutput, calls=%fused_computation.13.clone.1 | convolution fusion | flops 14189568 | bytes 1657856 | tf_op jit(solution)/shard_map/while/body/eval_jaxpr/...aun,...san->...sau/dot_general | solution.py:65
  92.3 3.4 %collective-permute-start.4 = (f32[3,128]{1,0:T(4,128)S(1)}, f32[3,128]{1,0:T(4,128)S(1)}, u32[]{:S(2)}, u32[]{:S(2)}) collective-permute-start(f32[3,128]{1,0:T(4,128)S(1)} %slice_bitcast_fusion), channel_id=1, source_target_pairs={{0,8},{8,16},{16,24},{1,9},{9,17},{17,25},{2,10},{10,18},{18,26},{... | collective-permute-start | bytes 4616 | tf_op jit(solution)/shard_map/ppermute | solution.py:40
  97.0 0.6 dynamic-slice
  97.6 1.9 %collective-permute-start.7 = (f32[1,3,1024]{2,1,0:T(4,128)S(1)}, f32[1,3,1024]{2,1,0:T(4,128)S(1)}, u32[]{:S(2)}, u32[]{:S(2)}) collective-permute-start(f32[1,3,1024]{2,1,0:T(4,128)S(1)} %get-tuple-element.123), channel_id=1, source_target_pairs={{0,8},{8,16},{16,24},{1,9},{9,17},{17,25},{2,10},{10,18},{18,26},{... | collective-permute-start | bytes 36872 | tf_op jit(solution)/shard_map/ppermute | solution.py:28
  99.5 4.8 %collective-permute-start.8 = (f32[1,3,1024]{2,1,0:T(4,128)S(1)}, f32[1,3,1024]{2,1,0:T(4,128)S(1)}, u32[]{:S(2)}, u32[]{:S(2)}) collective-permute-start(f32[1,3,1024]{2,1,0:T(4,128)S(1)} %get-tuple-element.123), channel_id=1, source_target_pairs={{8,0},{16,8},{24,16},{9,1},{17,9},{25,17},{10,2},{18,10},{26,18},{... | collective-permute-start | bytes 36872 | tf_op jit(solution)/shard_map/ppermute | solution.py:30
  104.4 0.6 fusion.36
  105.0 16.9 %psum.14 = f32[1]{0:T(128)} all-reduce(f32[1]{0:T(128)} %bitcast.9), channel_id=1, replica_groups=mesh['image'=4,'space'=8] {'space'}, use_global_device_ids=true, to_apply=%region_9.10 | all-reduce | flops 1 | bytes 8 | tf_op jit(solution)/shard_map/psum | solution.py:132
  122.9 1.3 dynamic-update-slice
  124.2 8.7 %all-reduce.1 = (f32[1]{0:T(128)}, f32[4]{0:T(128)S(1)}) all-reduce(f32[1]{0:T(128)} %sqrt_select_fusion, f32[4]{0:T(128)S(1)} %dynamic-update-slice), channel_id=1, replica_groups=mesh['image'=4,'space'=8] {'image'}, use_global_device_ids=true, to_apply=%region_10.11 | all-reduce | flops 5 | bytes 40 | tf_op jit(solution)/shard_map/psum | solution.py:139
  132.8 3.7 %while.24 = (s32[]{:T(128)}, f32[]{:T(128)}, s32[]{:T(128)}, f32[4]{0:T(128)S(1)}, s32[]{:T(128)}) while((s32[]{:T(128)}, f32[]{:T(128)}, s32[]{:T(128)}, f32[4]{0:T(128)S(1)}, s32[]{:T(128)}) %tuple.67), condition=%wide.region_12.13_spmd, body=%wide.region_11.12_spmd.sunk | while | flops 5 | bytes 107 | solution.py:52
  132.8 0.6 dynamic_slice.13
  134.1 0.6 dynamic_slice.13
  135.3 0.6 dynamic_slice.13
  137.1 4.6 %collective-permute-start.5 = (f32[1]{0:T(128)}, f32[1]{0:T(128)}, u32[]{:S(2)}, u32[]{:S(2)}) collective-permute-start(f32[1]{0:T(128)} %add.276), channel_id=1, source_target_pairs={{0,8},{8,16},{16,24},{1,9},{9,17},{17,25},{2,10},{10,18},{18,26},{... | collective-permute-start | bytes 20 | tf_op jit(solution)/shard_map/ppermute | solution.py:28
  141.8 4.7 %collective-permute-start.6 = (f32[1]{0:T(128)}, f32[1]{0:T(128)}, u32[]{:S(2)}, u32[]{:S(2)}) collective-permute-start(f32[1]{0:T(128)} %add.276), channel_id=1, source_target_pairs={{8,0},{16,8},{24,16},{9,1},{17,9},{25,17},{10,2},{18,10},{26,18},{... | collective-permute-start | bytes 20 | tf_op jit(solution)/shard_map/ppermute | solution.py:30
  147.8 2.0 %fusion.40 = (f32[]{:T(128)}, f32[]{:T(128)}) fusion(s32[]{:T(128)} %bitcast.16, s32[]{:T(128)} %bitcast.2, f32[1,1]{1,0:T(1,128)} %bitcast.14, f32[1,1]{1,0:T(1,128)} %bitcast.13, f32[1,1]{1,0:T(1,128)} %bitcast.12), kind=kLoop, calls=%fused_computation.89 | loop fusion | flops 22 | bytes 28 | tf_op jit(solution)/shard_map/reduce_sum | solution.py:149
  151.9 0.6 dot_general.22
  (176 shorter events, 7.2 us)
Async XLA Ops:
  1.3 7.4 %collective-permute-start.2 = (f32[1,3,512]{2,0,1:T(1,128)S(1)}, f32[1,3,512]{2,0,1:T(1,128)S(1)}, u32[]{:S(2)}, u32[]{:S(2)}) collective-permute-start(f32[1,3,512]{2,0,1:T(1,128)S(1)} %get-tuple-element.208), channel_id=1, source_target_pairs={{0,1},{1,2},{2,3},{3,4},{4,5},{5,6},{6,7},{7,0},{8,9},{9,10},{10,1... | collective-permute-start | bytes 18440 | tf_op jit(solution)/shard_map/ppermute | solution.py:28
  1.3 7.4 %collective-permute-start.3 = (f32[1,3,512]{2,0,1:T(1,128)S(1)}, f32[1,3,512]{2,0,1:T(1,128)S(1)}, u32[]{:S(2)}, u32[]{:S(2)}) collective-permute-start(f32[1,3,512]{2,0,1:T(1,128)S(1)} %get-tuple-element.209), channel_id=1, source_target_pairs={{1,0},{2,1},{3,2},{4,3},{5,4},{6,5},{7,6},{0,7},{9,8},{10,9},{11,1... | collective-permute-start | bytes 18440 | tf_op jit(solution)/shard_map/ppermute | solution.py:30
  9.6 87.4 %copy-start = (u32[32]{0:T(128)S(1)}, u32[32]{0:T(128)}, u32[]{:S(2)}) copy-start(u32[32]{0:T(128)} %constant.168) | copy-start | bytes 388
  9.6 4.9 %collective-permute-start = (f32[1,3,512]{2,1,0:T(4,128)S(1)}, f32[1,3,512]{2,1,0:T(4,128)S(1)}, u32[]{:S(2)}, u32[]{:S(2)}) collective-permute-start(f32[1,3,512]{2,1,0:T(4,128)S(1)} %get-tuple-element.284), channel_id=1, source_target_pairs={{0,1},{1,2},{2,3},{3,4},{4,5},{5,6},{6,7},{7,0},{8,9},{9,10},{10,1... | collective-permute-start | bytes 18440 | tf_op jit(solution)/shard_map/while/body/eval_jaxpr/ppermute | solution.py:28
  9.7 4.9 %collective-permute-start.1 = (f32[1,3,512]{2,1,0:T(4,128)S(1)}, f32[1,3,512]{2,1,0:T(4,128)S(1)}, u32[]{:S(2)}, u32[]{:S(2)}) collective-permute-start(f32[1,3,512]{2,1,0:T(4,128)S(1)} %get-tuple-element.285), channel_id=1, source_target_pairs={{1,0},{2,1},{3,2},{4,3},{5,4},{6,5},{7,6},{0,7},{9,8},{10,9},{11,1... | collective-permute-start | bytes 18440 | tf_op jit(solution)/shard_map/while/body/eval_jaxpr/ppermute | solution.py:30
  26.1 4.9 %collective-permute-start = (f32[1,3,512]{2,1,0:T(4,128)S(1)}, f32[1,3,512]{2,1,0:T(4,128)S(1)}, u32[]{:S(2)}, u32[]{:S(2)}) collective-permute-start(f32[1,3,512]{2,1,0:T(4,128)S(1)} %get-tuple-element.284), channel_id=1, source_target_pairs={{0,1},{1,2},{2,3},{3,4},{4,5},{5,6},{6,7},{7,0},{8,9},{9,10},{10,1... | collective-permute-start | bytes 18440 | tf_op jit(solution)/shard_map/while/body/eval_jaxpr/ppermute | solution.py:28
  26.2 4.9 %collective-permute-start.1 = (f32[1,3,512]{2,1,0:T(4,128)S(1)}, f32[1,3,512]{2,1,0:T(4,128)S(1)}, u32[]{:S(2)}, u32[]{:S(2)}) collective-permute-start(f32[1,3,512]{2,1,0:T(4,128)S(1)} %get-tuple-element.285), channel_id=1, source_target_pairs={{1,0},{2,1},{3,2},{4,3},{5,4},{6,5},{7,6},{0,7},{9,8},{10,9},{11,1... | collective-permute-start | bytes 18440 | tf_op jit(solution)/shard_map/while/body/eval_jaxpr/ppermute | solution.py:30
  42.6 4.9 %collective-permute-start = (f32[1,3,512]{2,1,0:T(4,128)S(1)}, f32[1,3,512]{2,1,0:T(4,128)S(1)}, u32[]{:S(2)}, u32[]{:S(2)}) collective-permute-start(f32[1,3,512]{2,1,0:T(4,128)S(1)} %get-tuple-element.284), channel_id=1, source_target_pairs={{0,1},{1,2},{2,3},{3,4},{4,5},{5,6},{6,7},{7,0},{8,9},{9,10},{10,1... | collective-permute-start | bytes 18440 | tf_op jit(solution)/shard_map/while/body/eval_jaxpr/ppermute | solution.py:28
  42.7 4.9 %collective-permute-start.1 = (f32[1,3,512]{2,1,0:T(4,128)S(1)}, f32[1,3,512]{2,1,0:T(4,128)S(1)}, u32[]{:S(2)}, u32[]{:S(2)}) collective-permute-start(f32[1,3,512]{2,1,0:T(4,128)S(1)} %get-tuple-element.285), channel_id=1, source_target_pairs={{1,0},{2,1},{3,2},{4,3},{5,4},{6,5},{7,6},{0,7},{9,8},{10,9},{11,1... | collective-permute-start | bytes 18440 | tf_op jit(solution)/shard_map/while/body/eval_jaxpr/ppermute | solution.py:30
  59.2 4.9 %collective-permute-start = (f32[1,3,512]{2,1,0:T(4,128)S(1)}, f32[1,3,512]{2,1,0:T(4,128)S(1)}, u32[]{:S(2)}, u32[]{:S(2)}) collective-permute-start(f32[1,3,512]{2,1,0:T(4,128)S(1)} %get-tuple-element.284), channel_id=1, source_target_pairs={{0,1},{1,2},{2,3},{3,4},{4,5},{5,6},{6,7},{7,0},{8,9},{9,10},{10,1... | collective-permute-start | bytes 18440 | tf_op jit(solution)/shard_map/while/body/eval_jaxpr/ppermute | solution.py:28
  59.2 4.9 %collective-permute-start.1 = (f32[1,3,512]{2,1,0:T(4,128)S(1)}, f32[1,3,512]{2,1,0:T(4,128)S(1)}, u32[]{:S(2)}, u32[]{:S(2)}) collective-permute-start(f32[1,3,512]{2,1,0:T(4,128)S(1)} %get-tuple-element.285), channel_id=1, source_target_pairs={{1,0},{2,1},{3,2},{4,3},{5,4},{6,5},{7,6},{0,7},{9,8},{10,9},{11,1... | collective-permute-start | bytes 18440 | tf_op jit(solution)/shard_map/while/body/eval_jaxpr/ppermute | solution.py:30
  75.7 4.9 %collective-permute-start = (f32[1,3,512]{2,1,0:T(4,128)S(1)}, f32[1,3,512]{2,1,0:T(4,128)S(1)}, u32[]{:S(2)}, u32[]{:S(2)}) collective-permute-start(f32[1,3,512]{2,1,0:T(4,128)S(1)} %get-tuple-element.284), channel_id=1, source_target_pairs={{0,1},{1,2},{2,3},{3,4},{4,5},{5,6},{6,7},{7,0},{8,9},{9,10},{10,1... | collective-permute-start | bytes 18440 | tf_op jit(solution)/shard_map/while/body/eval_jaxpr/ppermute | solution.py:28
  75.8 4.9 %collective-permute-start.1 = (f32[1,3,512]{2,1,0:T(4,128)S(1)}, f32[1,3,512]{2,1,0:T(4,128)S(1)}, u32[]{:S(2)}, u32[]{:S(2)}) collective-permute-start(f32[1,3,512]{2,1,0:T(4,128)S(1)} %get-tuple-element.285), channel_id=1, source_target_pairs={{1,0},{2,1},{3,2},{4,3},{5,4},{6,5},{7,6},{0,7},{9,8},{10,9},{11,1... | collective-permute-start | bytes 18440 | tf_op jit(solution)/shard_map/while/body/eval_jaxpr/ppermute | solution.py:30
  92.3 12.1 %collective-permute-start.4 = (f32[3,128]{1,0:T(4,128)S(1)}, f32[3,128]{1,0:T(4,128)S(1)}, u32[]{:S(2)}, u32[]{:S(2)}) collective-permute-start(f32[3,128]{1,0:T(4,128)S(1)} %slice_bitcast_fusion), channel_id=1, source_target_pairs={{0,8},{8,16},{16,24},{1,9},{9,17},{17,25},{2,10},{10,18},{18,26},{... | collective-permute-start | bytes 4616 | tf_op jit(solution)/shard_map/ppermute | solution.py:40
  97.6 54.1 %collective-permute-start.7 = (f32[1,3,1024]{2,1,0:T(4,128)S(1)}, f32[1,3,1024]{2,1,0:T(4,128)S(1)}, u32[]{:S(2)}, u32[]{:S(2)}) collective-permute-start(f32[1,3,1024]{2,1,0:T(4,128)S(1)} %get-tuple-element.123), channel_id=1, source_target_pairs={{0,8},{8,16},{16,24},{1,9},{9,17},{17,25},{2,10},{10,18},{18,26},{... | collective-permute-start | bytes 36872 | tf_op jit(solution)/shard_map/ppermute | solution.py:28
  99.5 52.1 %collective-permute-start.8 = (f32[1,3,1024]{2,1,0:T(4,128)S(1)}, f32[1,3,1024]{2,1,0:T(4,128)S(1)}, u32[]{:S(2)}, u32[]{:S(2)}) collective-permute-start(f32[1,3,1024]{2,1,0:T(4,128)S(1)} %get-tuple-element.123), channel_id=1, source_target_pairs={{8,0},{16,8},{24,16},{9,1},{17,9},{25,17},{10,2},{18,10},{26,18},{... | collective-permute-start | bytes 36872 | tf_op jit(solution)/shard_map/ppermute | solution.py:30
  137.1 10.6 %collective-permute-start.5 = (f32[1]{0:T(128)}, f32[1]{0:T(128)}, u32[]{:S(2)}, u32[]{:S(2)}) collective-permute-start(f32[1]{0:T(128)} %add.276), channel_id=1, source_target_pairs={{0,8},{8,16},{16,24},{1,9},{9,17},{17,25},{2,10},{10,18},{18,26},{... | collective-permute-start | bytes 20 | tf_op jit(solution)/shard_map/ppermute | solution.py:28
  141.8 6.0 %collective-permute-start.6 = (f32[1]{0:T(128)}, f32[1]{0:T(128)}, u32[]{:S(2)}, u32[]{:S(2)}) collective-permute-start(f32[1]{0:T(128)} %add.276), channel_id=1, source_target_pairs={{8,0},{16,8},{24,16},{9,1},{17,9},{25,17},{10,2},{18,10},{26,18},{... | collective-permute-start | bytes 20 | tf_op jit(solution)/shard_map/ppermute | solution.py:30
where the time goes:
time: 156 us; the launch traced here: 154 us
  matrix products  50 us (32%)
  starting transfers between devices  41 us (26%)
  blocking collectives  25.5 us (16%)
  local copies, waits for them, and re-layouts  18.6 us (12%)
  between operations  8.09 us (5%)
  other arithmetic  5.26 us (3%)
  waiting for transfers between devices  2.63 us (2%)
  loops' own time  2.51 us (2%)
    ppermute x8, starting transfers between devices, extended(): lax.ppermute(head, axis, [((i + 1) % count, i) for i in range(ends)])  30.8 us
    dot_general x10, matrix products, pair_forces(): jnp.einsum('...euh,...euw->...uhw', swarm_centres, partner_beads, precisi...  27.8 us
    dot_general x10, matrix products, pair_forces(): jnp.einsum('...aun,...san->...sau', weight_factors, partner_beads, precis...  22 us
    psum x1, blocking collectives, body(): squares = lax.psum(partial_value, 'space')  16.9 us
    psum x1, blocking collectives, body(): length_total = lax.psum(running[per_device - 1], 'image')  8.66 us
    ppermute x8, starting transfers between devices, extended(): lax.ppermute(tail, axis, [(i, (i + 1) % count) for i in range(ends)])  6.84 us
    gather x10, local copies, waits for them, and re-layouts, block_forces(): partners = jnp.take(widened, partner_rows, axis=-2)  6.03 us
    unnamed x10, local copies, waits for them, and re-layouts  4.2 us
  transfers between devices with their start and end apart: 17, of which 9 were waited for; matrix products, arithmetic and copies ran while one was open for 9% of the time, Pallas kernels for 0%

commit v1 on v0

v1 whole, which is shorter than its diff:
```python
import functools
import math

import jax
import jax.numpy as jnp
from jax import lax
from jax.experimental import pallas as pl
from jax.experimental.pallas import tpu as pltpu
from jax.sharding import PartitionSpec as P

PROT_DEV = 128
BLOCK = 128
HALO = 2
STEPS = 10

TIME_STEP = 0.05
RESTRAINT = 1.0
COUPLING = 3.0
KERNEL_RATE = 0.125
EPSILON = 1e-06
CODE_SCALE = 65536.0

SCALE = math.sqrt(2.0 * KERNEL_RATE * math.log2(math.e))
ROWS = 8
SUB = 8
GROUP = 4


def parts_of(v):
    first = v.astype(jnp.bfloat16).astype(jnp.float32)
    rest = v - first
    second = rest.astype(jnp.bfloat16).astype(jnp.float32)
    return first, second, rest - second


def row_ids():
    return lax.broadcasted_iota(jnp.int32, (ROWS, BLOCK), 0)


def place(u, block, half, state, left_feat, right_feat, columns):
    rows = row_ids()
    u = jnp.where(rows < 3, u, 0.0)
    norm = -0.5 * jnp.sum(u * u, axis=0, keepdims=True)
    left = jnp.where(rows == 3, norm, jnp.where(rows == 4, 1.0, u))
    right = jnp.where(rows == 4, norm, jnp.where(rows == 3, 1.0, u))
    state[half, block] = u
    l1, l2, l3 = parts_of(left)
    r1, r2, r3 = parts_of(right)
    zero = jnp.zeros_like(u)
    stacked = jnp.concatenate([l1, l1, l2, l2, l1, l3, zero, zero], axis=0)
    left_feat[half, block] = stacked.T.astype(jnp.bfloat16)
    right_feat[half, block] = jnp.concatenate([r1, r2, r1, r2, r3, r1, zero, zero], axis=0).astype(jnp.bfloat16)
    tall = u.T
    for c in range(3):
        columns[half, block, c] = jnp.broadcast_to(tall[:, c : c + 1], (BLOCK, BLOCK))


def evolve_kernel(
    near, own_blocks, blocks, copies,
    table, slabs, out, shared,
    state, first, left_feat, right_feat, columns,
):
    slab = lax.axis_index("space")
    count = slabs.shape[0]
    total = count * own_blocks
    reach = HALO * STEPS

    def load(block, carry):
        spot = block + (near * own_blocks - reach)
        source = lax.rem(slab + spot // own_blocks + (count * near - near), count)
        lane = pl.multiple_of(lax.rem(spot, own_blocks) * BLOCK, BLOCK)
        x = slabs[source, :, pl.ds(lane, BLOCK)]
        u = jnp.concatenate([x * SCALE, jnp.zeros((ROWS - 3, BLOCK), jnp.float32)], axis=0)
        first[block] = u
        place(u, block, 0, state, left_feat, right_feat, columns)
        return carry

    lax.fori_loop(0, blocks, load, 0)

    def centre(block, half, last):
        row = lax.rem(slab * own_blocks + block + (total * 4 - reach), total)
        partners = table.shape[1]
        right = right_feat[half, block]
        sums = [jnp.zeros((SUB, BLOCK), jnp.float32) for _ in range(4)]
        for k in range(partners):
            other = block + table[row, k] - HALO
            power = lax.dot_general(
                left_feat[half, other], right, (((1,), (0,)), ((), ())),
                preferred_element_type=jnp.float32,
            )
            w = jnp.exp2(power)
            for r in range(0, BLOCK, SUB):
                piece = w[r : r + SUB]
                sums[3] = sums[3] + piece
                for c in range(3):
                    sums[c] = sums[c] + piece * columns[half, other, c, pl.ds(r, SUB)]
        rows = row_ids()
        sx, sy, sz, sw = [jnp.sum(s, axis=0, keepdims=True) for s in sums]
        pulled = jnp.where(rows == 0, sx, jnp.where(rows == 1, sy, sz))
        u = state[half, block]
        force = (COUPLING / (partners * BLOCK)) * (u * sw - pulled)
        spot = lax.rem(block + (own_blocks * STEPS - reach), own_blocks)
        hold = jnp.where(spot * BLOCK < PROT_DEV, RESTRAINT, 0.0)
        return u + TIME_STEP * (force - hold * (u - first[block]))

    def step(turn, carry):
        half = lax.rem(turn, 2)
        low = HALO * (turn + 1)
        groups = (blocks - 2 * low) // GROUP

        def group(index, inner):
            base = low + index * GROUP
            new = [centre(base + g, half, False) for g in range(GROUP)]
            for g in range(GROUP):
                place(new[g], base + g, 1 - half, state, left_feat, right_feat, columns)
            return inner

        lax.fori_loop(0, groups, group, 0)
        return carry

    lax.fori_loop(0, STEPS, step, 0)
    last = STEPS % 2
    for a in range(own_blocks):
        out[0, :, a * BLOCK : (a + 1) * BLOCK] = state[last, reach + a, :3] * (1.0 / SCALE)
    protein = out[0, :, :PROT_DEV]

    def spread(index, carry):
        shared[index] = protein
        return carry

    lax.fori_loop(0, copies, spread, 0)


def blend_kernel(images, slabs, brackets, codes, own, before, after, proteins, out, fraction):
    here = lax.axis_index("image")
    lower = brackets[0]
    zero = jnp.zeros((1, 1), jnp.float32)
    arcs = [zero]
    for k in range(1, images):
        d = proteins[k * slabs : (k + 1) * slabs] - proteins[(k - 1) * slabs : k * slabs]
        square = jnp.sum(jnp.sum(d * d, axis=0), axis=0, keepdims=True)
        square = jnp.sum(square, axis=1, keepdims=True)
        arcs.append(arcs[-1] + jnp.sqrt(square + EPSILON))
    total = arcs[-1]
    arc_here, arc_lower, arc_upper = zero, zero, zero
    for k in range(images):
        arc_here = jnp.where(here == k, arcs[k], arc_here)
        arc_lower = jnp.where(lower == k, arcs[k], arc_lower)
        arc_upper = jnp.where(lower + 1 == k, arcs[k], arc_upper)
    base = jnp.full((1, 1), lower, jnp.int32).astype(jnp.float32)
    code = jnp.full((1, 1), codes[0], jnp.int32).astype(jnp.float32)
    target = (base + code / CODE_SCALE) / (images - 1)
    weight = (target * total - arc_lower) / (arc_upper - arc_lower)
    mine, previous, following = own[0], before[0], after[0]
    below = jnp.where(lower == here, mine, previous)
    above = jnp.where(lower == here, following, mine)
    out[0] = (1.0 - weight) * below + weight * above
    fraction[...] = arc_here / total


def body(positions, neighbours, brackets, codes):
    slab_beads = positions.shape[2]
    own_blocks = slab_beads // BLOCK
    slabs = lax.axis_size("space")
    images = lax.axis_size("image")
    devices = slabs * images
    reach = HALO * STEPS
    blocks = own_blocks + 2 * reach
    near = -(-reach // own_blocks)
    vmem = pl.BlockSpec(memory_space=pltpu.VMEM)
    smem = pl.BlockSpec(memory_space=pltpu.SMEM)
    spread = jnp.broadcast_to(positions, (slabs,) + positions.shape[1:])
    around = lax.all_to_all(spread, "space", 0, 0, tiled=True)
    evolved, shared = pl.pallas_call(
        functools.partial(evolve_kernel, near, own_blocks, blocks, devices),
        out_shape=(
            jax.ShapeDtypeStruct(positions.shape, jnp.float32),
            jax.ShapeDtypeStruct((devices, 3, PROT_DEV), jnp.float32),
        ),
        in_specs=[smem, vmem],
        out_specs=(vmem, vmem),
        scratch_shapes=[
            pltpu.VMEM((2, blocks, ROWS, BLOCK), jnp.float32),
            pltpu.VMEM((blocks, ROWS, BLOCK), jnp.float32),
            pltpu.VMEM((2, blocks, BLOCK, 8 * ROWS), jnp.bfloat16),
            pltpu.VMEM((2, blocks, 8 * ROWS, BLOCK), jnp.bfloat16),
            pltpu.VMEM((2, blocks, 3, BLOCK, BLOCK), jnp.float32),
        ],
    )(neighbours, around)
    up = [(i, i + 1) for i in range(images - 1)]
    down = [(i + 1, i) for i in range(images - 1)]
    proteins = lax.all_to_all(shared, ("image", "space"), 0, 0, tiled=True)
    before = lax.ppermute(evolved, "image", up)
    after = lax.ppermute(evolved, "image", down)
    new_images, fraction = pl.pallas_call(
        functools.partial(blend_kernel, images, slabs),
        out_shape=(
            jax.ShapeDtypeStruct(positions.shape, jnp.float32),
            jax.ShapeDtypeStruct((1, 1), jnp.float32),
        ),
        in_specs=[smem, smem, vmem, vmem, vmem, vmem],
        out_specs=(vmem, vmem),
    )(brackets, codes, evolved, before, after, proteins)
    return new_images, fraction.reshape(1)


def solution(mesh):
    placed = (P("image", None, "space"), P(), P("image"), P("image"))
    return jax.shard_map(
        body,
        mesh=mesh,
        in_specs=placed,
        out_specs=(P("image", None, "space"), P("image")),
        check_vma=False,
    )
```

time: 156 us -> 105 us (0.67)
  the two profiles are of different devices: /device:TPU:4 before, /device:TPU:0 now
where the time goes in v1:
time: 105 us; the launch traced here: 104 us
  Pallas kernels  72.7 us (69%)
  starting transfers between devices  15.1 us (14%)
  waiting for transfers between devices  9.07 us (9%)
  local copies, waits for them, and re-layouts  5.28 us (5%)
  between operations  1.99 us (2%)
    pallas_call x1, Pallas kernels, body(): pl.pallas_call(functools.partial(evolve_kernel, near, own_blocks, blocks,...  71 us
    all_to_all x1, starting transfers between devices, body(): around = lax.all_to_all(spread, 'space', 0, 0, tiled=True)  6.49 us
    all_to_all x1, waiting for transfers between devices, body(): around = lax.all_to_all(spread, 'space', 0, 0, tiled=True)  6.05 us
    unnamed x15, local copies, waits for them, and re-layouts  4.61 us
    all_to_all x1, starting transfers between devices, body(): proteins = lax.all_to_all(shared, ('image', 'space'), 0, 0, tiled=True)  3.69 us
    ppermute x1, starting transfers between devices, body(): before = lax.ppermute(evolved, 'image', up)  3.67 us
    ppermute x1, waiting for transfers between devices, body(): after = lax.ppermute(evolved, 'image', down)  3.02 us
  transfers between devices with their start and end apart: 4, of which 2 were waited for; matrix products, arithmetic and copies ran while one was open for 1% of the time, Pallas kernels for 0%

profile of v1, /device:TPU:0, one launch (start us, length us, event | category | flops | bytes accessed | tf_op | source)
XLA Modules:
  0.0 104.1 jit_solution(1709651580128249512)
XLA Ops:
  0.6 0.7 copy.10
  1.3 0.7 broadcast_in_dim.8
  2.0 0.0 copy-start.5
  2.0 6.5 %all-to-all-start = ((f32[8,3,1024]{2,1,0:T(4,128)}), f32[8,3,1024]{2,1,0:T(4,128)S(1)}, u32[]{:S(2)}, u32[]{:S(2)}) async-start(f32[8,3,1024]{2,1,0:T(4,128)} %broadcast_in_dim.8), calls=%async_computation | async-start | bytes 262144 | tf_op jit(solution)/shard_map/all_to_all | solution.py:173
  8.5 0.0 copy-done.5
  8.5 0.7 copy.6.table
  9.2 6.0 %all-to-all-done.slabs = f32[8,3,1024]{2,1,0:T(4,128)S(1)} async-done(((f32[8,3,1024]{2,1,0:T(4,128)}), f32[8,3,1024]{2,1,0:T(4,128)S(1)}, u32[]{:S(2)}, u32[]{:S(2)}) %all-to-all-start) | async-done | bytes 98336 | tf_op jit(solution)/shard_map/all_to_all | solution.py:173
  15.2 0.0 copy-start
  15.2 0.6 copy-done
  15.9 71.0 %shard_map.59 = (f32[1,3,1024]{2,1,0:T(4,128)}, f32[32,3,128]{2,1,0:T(4,128)}) custom-call(s32[64,3]{1,0:T(8,128)} %copy.6.table, f32[8,3,1024]{2,1,0:T(4,128)} %copy-done), custom_call_target="tpu_custom_call" | custom-call | tf_op jit(solution)/shard_map/pallas_call | solution.py:174
  86.9 0.0 copy-start.2
  86.9 3.7 %all-to-all-start.1 = ((f32[32,3,128]{2,1,0:T(4,128)}), f32[32,3,128]{2,1,0:T(4,128)S(1)}, u32[]{:S(2)}, u32[]{:S(2)}) async-start(f32[32,3,128]{2,1,0:T(4,128)} %get-tuple-element.7), calls=%async_computation.1 | async-start | bytes 131072 | tf_op jit(solution)/shard_map/all_to_all | solution.py:192
  90.6 0.0 copy-done.2
  90.6 3.7 %collective-permute-start = (f32[1,3,1024]{2,1,0:T(4,128)S(1)}, f32[1,3,1024]{2,1,0:T(4,128)S(1)}, u32[]{:S(2)}, u32[]{:S(2)}) collective-permute-start(f32[1,3,1024]{2,1,0:T(4,128)S(1)} %copy-done.2), channel_id=1, source_target_pairs={{0,8},{8,16},{16,24},{1,9},{9,17},{17,25},{2,10},{10,18},{18,26},{... | collective-permute-start | bytes 36872 | tf_op jit(solution)/shard_map/ppermute | solution.py:193
  94.3 1.3 %collective-permute-start.1 = (f32[1,3,1024]{2,1,0:T(4,128)S(1)}, f32[1,3,1024]{2,1,0:T(4,128)S(1)}, u32[]{:S(2)}, u32[]{:S(2)}) collective-permute-start(f32[1,3,1024]{2,1,0:T(4,128)S(1)} %copy-done.2), channel_id=1, source_target_pairs={{8,0},{16,8},{24,16},{9,1},{17,9},{25,17},{10,2},{18,10},{26,18},{... | collective-permute-start | bytes 36872 | tf_op jit(solution)/shard_map/ppermute | solution.py:194
  96.9 0.0 collective-permute-done.before
  96.9 0.0 copy-start.3
  96.9 3.0 %collective-permute-done.1.after = f32[1,3,1024]{2,1,0:T(4,128)S(1)} collective-permute-done((f32[1,3,1024]{2,1,0:T(4,128)S(1)}, f32[1,3,1024]{2,1,0:T(4,128)S(1)}, u32[]{:S(2)}, u32[]{:S(2)}) %collective-permute-start.1) | collective-permute-done | bytes 12320 | tf_op jit(solution)/shard_map/ppermute | solution.py:194
  100.0 0.0 copy-start.4
  100.0 0.0 all-to-all-done.1.proteins
  100.0 0.0 copy-done.3
  100.0 0.6 copy-done.4
  100.6 0.0 copy-start.1
  100.6 0.6 copy-done.1
  101.2 1.6 %shard_map.60 = (f32[1,3,1024]{2,1,0:T(4,128)}, f32[1,1]{1,0:T(1,128)}) custom-call(s32[1]{0:T(128)S(6)} %copy.11.brackets, s32[1]{0:T(128)S(6)} %copy.12.codes, f32[1,3,1024]{2,1,0:T(4,128)} %get-tuple-element.6.own, f32[1,3,1024]{2,1,0:T(4,128)} %copy-done.3, f32[1,3,1024]{2,1,0:T(4,128)} %copy-done.4, f32[32,3,128]{2,1,0:T(4,128)} %copy-done.1), custom_call_target="tpu_custom_call" | custom-call | tf_op jit(solution)/shard_map/pallas_call | solution.py:195
  102.8 1.3 %copy.7 = f32[1,3,1024]{2,0,1:T(1,128)} copy(f32[1,3,1024]{2,1,0:T(4,128)} %get-tuple-element.10) | data formatting | bytes 24576
Async XLA Ops:
  2.0 6.5 %copy-start.5 = (s32[64,3]{0,1:T(4,128)S(1)}, s32[64,3]{0,1:T(4,128)}, u32[]{:S(2)}) copy-start(s32[64,3]{0,1:T(4,128)} %param.5) | copy-start | bytes 2308
  2.0 13.2 %all-to-all-start = ((f32[8,3,1024]{2,1,0:T(4,128)}), f32[8,3,1024]{2,1,0:T(4,128)S(1)}, u32[]{:S(2)}, u32[]{:S(2)}) async-start(f32[8,3,1024]{2,1,0:T(4,128)} %broadcast_in_dim.8), calls=%async_computation | async-start | bytes 262144 | tf_op jit(solution)/shard_map/all_to_all | solution.py:173
  15.2 0.7 copy-start
  86.9 3.7 %copy-start.2 = (f32[1,3,1024]{2,1,0:T(4,128)S(1)}, f32[1,3,1024]{2,1,0:T(4,128)}, u32[]{:S(2)}) copy-start(f32[1,3,1024]{2,1,0:T(4,128)} %get-tuple-element.6.own) | copy-start | bytes 36868
  86.9 13.0 %all-to-all-start.1 = ((f32[32,3,128]{2,1,0:T(4,128)}), f32[32,3,128]{2,1,0:T(4,128)S(1)}, u32[]{:S(2)}, u32[]{:S(2)}) async-start(f32[32,3,128]{2,1,0:T(4,128)} %get-tuple-element.7), calls=%async_computation.1 | async-start | bytes 131072 | tf_op jit(solution)/shard_map/all_to_all | solution.py:192
  90.6 6.3 %collective-permute-start = (f32[1,3,1024]{2,1,0:T(4,128)S(1)}, f32[1,3,1024]{2,1,0:T(4,128)S(1)}, u32[]{:S(2)}, u32[]{:S(2)}) collective-permute-start(f32[1,3,1024]{2,1,0:T(4,128)S(1)} %copy-done.2), channel_id=1, source_target_pairs={{0,8},{8,16},{16,24},{1,9},{9,17},{17,25},{2,10},{10,18},{18,26},{... | collective-permute-start | bytes 36872 | tf_op jit(solution)/shard_map/ppermute | solution.py:193
  94.3 5.6 %collective-permute-start.1 = (f32[1,3,1024]{2,1,0:T(4,128)S(1)}, f32[1,3,1024]{2,1,0:T(4,128)S(1)}, u32[]{:S(2)}, u32[]{:S(2)}) collective-permute-start(f32[1,3,1024]{2,1,0:T(4,128)S(1)} %copy-done.2), channel_id=1, source_target_pairs={{8,0},{16,8},{24,16},{9,1},{17,9},{25,17},{10,2},{18,10},{26,18},{... | collective-permute-start | bytes 36872 | tf_op jit(solution)/shard_map/ppermute | solution.py:194
  96.9 3.0 %copy-start.3 = (f32[1,3,1024]{2,1,0:T(4,128)}, f32[1,3,1024]{2,1,0:T(4,128)S(1)}, u32[]{:S(2)}) copy-start(f32[1,3,1024]{2,1,0:T(4,128)S(1)} %collective-permute-done.before) | copy-start | bytes 36868
  100.0 0.6 copy-start.4
  100.6 0.6 copy-start.1

commit v2 on v1

v2 whole, which is shorter than its diff:
```python
import functools
import math

import jax
import jax.numpy as jnp
from jax import lax
from jax.experimental import pallas as pl
from jax.experimental.pallas import tpu as pltpu
from jax.sharding import PartitionSpec as P

PROT_DEV = 128
BLOCK = 128
HALO = 2
STEPS = 10

TIME_STEP = 0.05
RESTRAINT = 1.0
COUPLING = 3.0
KERNEL_RATE = 0.125
EPSILON = 1e-06
CODE_SCALE = 65536.0

SCALE = math.sqrt(2.0 * KERNEL_RATE * math.log2(math.e))
ROWS = 8
SUB = 8
GROUP = 4
PAD = GROUP
PHASES = (6, 4)


def parts_of(v):
    first = v.astype(jnp.bfloat16).astype(jnp.float32)
    rest = v - first
    second = rest.astype(jnp.bfloat16).astype(jnp.float32)
    return first, second, rest - second


def row_ids():
    return lax.broadcasted_iota(jnp.int32, (ROWS, BLOCK), 0)


def spread_matrix():
    row = lax.broadcasted_iota(jnp.int32, (8 * ROWS, 3 * BLOCK), 0)
    column = lax.broadcasted_iota(jnp.int32, (8 * ROWS, 3 * BLOCK), 1) // BLOCK
    chosen = (row == column) | (row == column + 2 * ROWS) | (row == column + 5 * ROWS)
    return jnp.where(chosen, 1.0, 0.0).astype(jnp.bfloat16)


def place(u, block, refs, picks):
    state, left_feat, right_feat, columns = refs
    rows = row_ids()
    u = jnp.where(rows < 3, u, 0.0)
    norm = -0.5 * jnp.sum(u * u, axis=0, keepdims=True)
    left = jnp.where(rows == 3, norm, jnp.where(rows == 4, 1.0, u))
    right = jnp.where(rows == 4, norm, jnp.where(rows == 3, 1.0, u))
    state[block] = u
    l1, l2, l3 = parts_of(left)
    r1, r2, r3 = parts_of(right)
    zero = jnp.zeros_like(u)
    stacked = jnp.concatenate([l1, l1, l2, l2, l1, l3, zero, zero], axis=0)
    tall = stacked.T.astype(jnp.bfloat16)
    left_feat[block] = tall
    right_feat[block] = jnp.concatenate([r1, r2, r1, r2, r3, r1, zero, zero], axis=0).astype(jnp.bfloat16)
    columns[block] = lax.dot_general(
        tall, picks[...], (((1,), (0,)), ((), ())), preferred_element_type=jnp.float32
    )


def evolve_kernel(
    steps, near, copies, table, *refs,
):
    slabs, refs = refs[: 2 * near + 1], refs[2 * near + 1 :]
    if copies:
        anchors, refs = refs[: 2 * near + 1], refs[2 * near + 1 :]
        out, shared, refs = refs[0], refs[1], refs[2:]
    else:
        anchors, out, refs = slabs, refs[0], refs[1:]
    first, picks, even, odd = refs[0], refs[1], refs[2:6], refs[6:]
    own_blocks = out.shape[1]
    partners = table.shape[0]
    total = table.shape[1]
    reach = HALO * steps
    blocks = own_blocks + 2 * reach
    slab = lax.axis_index("space")
    picks[...] = spread_matrix()
    filler = jnp.zeros((ROWS - 3, BLOCK), jnp.float32)

    def scaled(ref, block):
        return jnp.concatenate([ref[:, block, :] * SCALE, filler], axis=0)

    for index in range(2 * near + 1):
        shift = (index - near) * own_blocks + reach
        begin, end = max(0, -shift), min(own_blocks, blocks - shift)

        def load(turn, carry, index=index, begin=begin, shift=shift):
            for g in range(GROUP):
                block = begin + turn * GROUP + g
                first[block + shift + PAD] = scaled(anchors[index], block)
                place(scaled(slabs[index], block), block + shift + PAD, even, picks)
            return carry

        lax.fori_loop(0, (end - begin) // GROUP, load, 0)

    def centre(block, source):
        state, left_feat, right_feat, columns = source
        spot = block - (PAD + reach)
        row = lax.rem(slab * own_blocks + spot + total, total)
        right = right_feat[block]
        sums = [jnp.zeros((SUB, BLOCK), jnp.float32) for _ in range(4)]
        for k in range(partners):
            other = block + table[k, row] - HALO
            power = lax.dot_general(
                left_feat[other], right, (((1,), (0,)), ((), ())),
                preferred_element_type=jnp.float32,
            )
            w = jnp.exp2(power)
            for r in range(0, BLOCK, SUB):
                piece = w[r : r + SUB]
                sums[3] = sums[3] + piece
                for c in range(3):
                    sums[c] = sums[c] + piece * columns[other, pl.ds(r, SUB), c * BLOCK : (c + 1) * BLOCK]
        rows = row_ids()
        sx, sy, sz, sw = [jnp.sum(s, axis=0, keepdims=True) for s in sums]
        pulled = jnp.where(rows == 0, sx, jnp.where(rows == 1, sy, sz))
        u = state[block]
        force = (COUPLING / (partners * BLOCK)) * (u * sw - pulled)
        inner = lax.rem(spot + own_blocks * near, own_blocks)
        hold = jnp.where(inner * BLOCK < PROT_DEV, RESTRAINT, 0.0)
        return u + TIME_STEP * (force - hold * (u - first[block]))

    def step(turn, source, target, final=False):
        low = HALO * (turn + 1) + PAD
        groups = (blocks + 2 * PAD - 2 * low) // GROUP

        def keep(new, base):
            for g in range(GROUP):
                if final:
                    target[0][base + g] = new[g]
                else:
                    place(new[g], base + g, target, picks)

        def group(index, held):
            base = low + index * GROUP
            keep(held, base - GROUP)
            return tuple(centre(base + g, source) for g in range(GROUP))

        start = tuple(jnp.zeros((ROWS, BLOCK), jnp.float32) for _ in range(GROUP))
        held = lax.fori_loop(0, groups, group, start)
        keep(held, low + (groups - 1) * GROUP)

    def both(pair, carry):
        step(2 * pair, even, odd)
        step(2 * pair + 1, odd, even)
        return carry

    lax.fori_loop(0, steps // 2 - 1, both, 0)
    step(steps - 2, even, odd)
    step(steps - 1, odd, even, True)
    for a in range(own_blocks):
        out[:, a, :] = even[0][PAD + reach + a, :3] * (1.0 / SCALE)
    if copies:
        protein = out[:, 0, :]

        def spread(index, carry):
            shared[index] = protein
            return carry

        lax.fori_loop(0, copies, spread, 0)


def blend_kernel(images, slabs, brackets, codes, own, before, after, proteins, out, fraction):
    here = lax.axis_index("image")
    lower = brackets[0]
    zero = jnp.zeros((1, 1), jnp.float32)
    arcs = [zero]
    for k in range(1, images):
        d = proteins[k * slabs : (k + 1) * slabs] - proteins[(k - 1) * slabs : k * slabs]
        square = jnp.sum(jnp.sum(d * d, axis=0), axis=0, keepdims=True)
        square = jnp.sum(square, axis=1, keepdims=True)
        arcs.append(arcs[-1] + jnp.sqrt(square + EPSILON))
    total = arcs[-1]
    arc_here, arc_lower, arc_upper = zero, zero, zero
    for k in range(images):
        arc_here = jnp.where(here == k, arcs[k], arc_here)
        arc_lower = jnp.where(lower == k, arcs[k], arc_lower)
        arc_upper = jnp.where(lower + 1 == k, arcs[k], arc_upper)
    base = jnp.full((1, 1), lower, jnp.int32).astype(jnp.float32)
    code = jnp.full((1, 1), codes[0], jnp.int32).astype(jnp.float32)
    target = (base + code / CODE_SCALE) / (images - 1)
    weight = (target * total - arc_lower) / (arc_upper - arc_lower)
    mine, previous, following = own[...], before[...], after[...]
    below = jnp.where(lower == here, mine, previous)
    above = jnp.where(lower == here, following, mine)
    weight = jnp.reshape(weight, (1, 1, 1))
    out[...] = (1.0 - weight) * below + weight * above
    fraction[...] = arc_here / total


VMEM = pl.BlockSpec(memory_space=pltpu.VMEM)
SMEM = pl.BlockSpec(memory_space=pltpu.SMEM)


def around(cells, near):
    count = lax.axis_size("space")
    found = []
    for distance in range(-near, near + 1):
        route = [((i + distance) % count, i) for i in range(count)]
        found.append(lax.ppermute(cells, "space", route) if distance else cells)
    return found


def evolve(steps, copies, table, slabs, anchors):
    shape = slabs[0].shape
    near = len(slabs) // 2
    blocks = shape[1] + 2 * HALO * steps + 2 * PAD
    outs = [jax.ShapeDtypeStruct(shape, jnp.float32)]
    if copies:
        outs.append(jax.ShapeDtypeStruct((copies, 3, PROT_DEV), jnp.float32))
    half = [
        pltpu.VMEM((blocks, ROWS, BLOCK), jnp.float32),
        pltpu.VMEM((blocks, BLOCK, 8 * ROWS), jnp.bfloat16),
        pltpu.VMEM((blocks, 8 * ROWS, BLOCK), jnp.bfloat16),
        pltpu.VMEM((blocks, BLOCK, 3 * BLOCK), jnp.float32),
    ]
    return pl.pallas_call(
        functools.partial(evolve_kernel, steps, near, copies),
        out_shape=outs,
        in_specs=[SMEM] + [VMEM] * (len(slabs) + len(anchors)),
        out_specs=[VMEM] * len(outs),
        scratch_shapes=[
            pltpu.VMEM((blocks, ROWS, BLOCK), jnp.float32),
            pltpu.VMEM((8 * ROWS, 3 * BLOCK), jnp.bfloat16),
            *half,
            *half,
        ],
        compiler_params=pltpu.CompilerParams(vmem_limit_bytes=32 << 20),
    )(table, *slabs, *anchors)


def body(positions, neighbours, brackets, codes):
    slabs = lax.axis_size("space")
    images = lax.axis_size("image")
    own_blocks = positions.shape[2] // BLOCK
    cells = positions.reshape(3, own_blocks, BLOCK)
    table = neighbours.T
    first = around(cells, -(-HALO * PHASES[0] // own_blocks))
    (middle,) = evolve(PHASES[0], 0, table, first, [])
    near = -(-HALO * PHASES[1] // own_blocks)
    skip = len(first) // 2 - near
    anchors = first[skip : len(first) - skip]
    evolved, shared = evolve(PHASES[1], slabs * images, table, around(middle, near), anchors)
    up = [(i, i + 1) for i in range(images - 1)]
    down = [(i + 1, i) for i in range(images - 1)]
    proteins = lax.all_to_all(shared, ("image", "space"), 0, 0, tiled=True)
    before = lax.ppermute(evolved, "image", up)
    after = lax.ppermute(evolved, "image", down)
    new_images, fraction = pl.pallas_call(
        functools.partial(blend_kernel, images, slabs),
        out_shape=(
            jax.ShapeDtypeStruct(cells.shape, jnp.float32),
            jax.ShapeDtypeStruct((1, 1), jnp.float32),
        ),
        in_specs=[SMEM, SMEM, VMEM, VMEM, VMEM, VMEM],
        out_specs=(VMEM, VMEM),
        compiler_params=pltpu.CompilerParams(vmem_limit_bytes=8 << 20),
    )(brackets, codes, evolved, before, after, proteins)
    return new_images.reshape(positions.shape), fraction.reshape(1)


def solution(mesh):
    placed = (P("image", None, "space"), P(), P("image"), P("image"))
    return jax.shard_map(
        body,
        mesh=mesh,
        in_specs=placed,
        out_specs=(P("image", None, "space"), P("image")),
        check_vma=False,
    )
```

time: 105 us -> 63.8 us (0.61)
  the two profiles are of different devices: /device:TPU:0 before, /device:TPU:4 now
where the time goes in v2:
time: 63.8 us; the launch traced here: 63.5 us
  Pallas kernels  34.3 us (54%)
  starting transfers between devices  14.3 us (22%)
  waiting for transfers between devices  12.2 us (19%)
  between operations  1.97 us (3%)
  local copies, waits for them, and re-layouts  0.72 us (1%)
    pallas_call x2, Pallas kernels, evolve(): pl.pallas_call(functools.partial(evolve_kernel, steps, near, copies), out...  33.6 us
    ppermute x6, waiting for transfers between devices, around(): found.append(lax.ppermute(cells, 'space', route) if distance else cells)  9.52 us
    ppermute x6, starting transfers between devices, around(): found.append(lax.ppermute(cells, 'space', route) if distance else cells)  5.4 us
    ppermute x1, starting transfers between devices, body(): after = lax.ppermute(evolved, 'image', down)  3.37 us
    all_to_all x1, starting transfers between devices, body(): proteins = lax.all_to_all(shared, ('image', 'space'), 0, 0, tiled=True)  3.03 us
    ppermute x1, waiting for transfers between devices, body(): before = lax.ppermute(evolved, 'image', up)  2.71 us
    ppermute x1, starting transfers between devices, body(): before = lax.ppermute(evolved, 'image', up)  2.47 us
  transfers between devices with their start and end apart: 9, of which 7 were waited for; matrix products, arithmetic and copies ran while one was open for 0% of the time, Pallas kernels for 0%

profile of v2, /device:TPU:4, one launch (start us, length us, event | category | flops | bytes accessed | tf_op | source)
XLA Modules:
  0.0 63.5 jit_solution(17436876670210008738)
XLA Ops:
  0.6 0.0 copy-start.2
  0.6 3.7 %collective-permute-start.3 = (f32[3,8,128]{2,1,0:T(8,128)}, f32[3,8,128]{2,1,0:T(8,128)S(1)}, u32[]{:S(2)}, u32[]{:S(2)}) collective-permute-start(f32[3,8,128]{2,1,0:T(8,128)} %bitcast.4), channel_id=1, source_target_pairs={{2,0},{3,1},{4,2},{5,3},{6,4},{7,5},{0,6},{1,7},{10,8},{11,9},{12,... | collective-permute-start | bytes 36872 | tf_op jit(solution)/shard_map/ppermute | solution.py:208
  4.3 0.0 collective-permute-start.2
  4.3 0.5 collective-permute-start.1
  4.8 0.7 %collective-permute-start = (f32[3,8,128]{2,1,0:T(8,128)}, f32[3,8,128]{2,1,0:T(8,128)S(1)}, u32[]{:S(2)}, u32[]{:S(2)}) collective-permute-start(f32[3,8,128]{2,1,0:T(8,128)} %bitcast.7), channel_id=1, source_target_pairs={{6,0},{7,1},{0,2},{1,3},{2,4},{3,5},{4,6},{5,7},{14,8},{15,9},{8,1... | collective-permute-start | bytes 36872 | tf_op jit(solution)/shard_map/ppermute | solution.py:208
  5.5 0.4 collective-permute-done.3.refs_4_
  5.9 0.1 collective-permute-done.2.refs_3_.refs_5_
  6.0 3.4 %collective-permute-done.1.refs_1_.refs_3_ = f32[3,8,128]{2,1,0:T(8,128)S(1)} collective-permute-done((f32[3,8,128]{2,1,0:T(8,128)}, f32[3,8,128]{2,1,0:T(8,128)S(1)}, u32[]{:S(2)}, u32[]{:S(2)}) %collective-permute-start.1) | collective-permute-done | bytes 12320 | tf_op jit(solution)/shard_map/ppermute | solution.py:208
  9.4 1.1 %collective-permute-done.refs_0_ = f32[3,8,128]{2,1,0:T(8,128)S(1)} collective-permute-done((f32[3,8,128]{2,1,0:T(8,128)}, f32[3,8,128]{2,1,0:T(8,128)S(1)}, u32[]{:S(2)}, u32[]{:S(2)}) %collective-permute-start) | collective-permute-done | bytes 12320 | tf_op jit(solution)/shard_map/ppermute | solution.py:208
  10.5 0.0 copy-done.2
  10.5 0.0 copy-start
  10.5 0.7 %copy-done = f32[1,3,1024]{2,0,1:T(1,128)S(1)} copy-done((f32[1,3,1024]{2,0,1:T(1,128)S(1)}, f32[1,3,1024]{2,0,1:T(1,128)}, u32[]{:S(2)}) %copy-start) | copy-done | bytes 12312
  11.2 0.0 copy-start.1
  11.2 21.0 %shard_map.59.refs_1_ = f32[3,8,128]{2,1,0:T(8,128)S(1)} custom-call(s32[3,64]{1,0:T(4,128)S(1)} %bitcast.10, f32[3,8,128]{2,1,0:T(8,128)S(1)} %collective-permute-done.refs_0_, f32[3,8,128]{2,1,0:T(8,128)S(1)} %collective-permute-done.1.refs_1_.refs_3_, f32[3,8,128]{2,1,0:T(8,128)S(1)} %bitcast.8, f32[3,8,128]{2,1,0:T(8,128)S(1)} %collective-permute-done.2.refs_3_.refs_5_, ...), custom_call_target="tpu_custom_call" | custom-call | tf_op jit(solution)/shard_map/pallas_call | solution.py:225
  32.2 0.1 collective-permute-start.5
  32.4 0.4 collective-permute-start.4
  32.8 1.0 %collective-permute-done.5.refs_2_ = f32[3,8,128]{2,1,0:T(8,128)S(1)} collective-permute-done((f32[3,8,128]{2,1,0:T(8,128)S(1)}, f32[3,8,128]{2,1,0:T(8,128)S(1)}, u32[]{:S(2)}, u32[]{:S(2)}) %collective-permute-start.5) | collective-permute-done | bytes 12320 | tf_op jit(solution)/shard_map/ppermute | solution.py:208
  33.8 3.5 %collective-permute-done.4.refs_0_ = f32[3,8,128]{2,1,0:T(8,128)S(1)} collective-permute-done((f32[3,8,128]{2,1,0:T(8,128)S(1)}, f32[3,8,128]{2,1,0:T(8,128)S(1)}, u32[]{:S(2)}, u32[]{:S(2)}) %collective-permute-start.4) | collective-permute-done | bytes 12320 | tf_op jit(solution)/shard_map/ppermute | solution.py:208
  37.3 0.0 copy-done.1
  37.3 12.6 %shard_map.60 = (f32[3,8,128]{2,1,0:T(8,128)S(1)}, f32[32,3,128]{2,1,0:T(4,128)}) custom-call(s32[3,64]{1,0:T(4,128)S(1)} %bitcast.11, f32[3,8,128]{2,1,0:T(8,128)S(1)} %collective-permute-done.4.refs_0_, f32[3,8,128]{2,1,0:T(8,128)S(1)} %shard_map.59.refs_1_, f32[3,8,128]{2,1,0:T(8,128)S(1)} %collective-permute-done.5.refs_2_, ...), custom_call_target="tpu_custom_call" | custom-call | tf_op jit(solution)/shard_map/pallas_call | solution.py:225
  49.9 3.0 %all-to-all-start = ((f32[32,3,128]{2,1,0:T(4,128)}), f32[32,3,128]{2,1,0:T(4,128)S(1)}, u32[]{:S(2)}, u32[]{:S(2)}) async-start(f32[32,3,128]{2,1,0:T(4,128)} %get-tuple-element.7), calls=%async_computation | async-start | bytes 131072 | tf_op jit(solution)/shard_map/all_to_all | solution.py:254
  52.9 3.4 %collective-permute-start.7 = (f32[3,8,128]{2,1,0:T(8,128)S(1)}, f32[3,8,128]{2,1,0:T(8,128)S(1)}, u32[]{:S(2)}, u32[]{:S(2)}) collective-permute-start(f32[3,8,128]{2,1,0:T(8,128)S(1)} %get-tuple-element.6.own), channel_id=1, source_target_pairs={{8,0},{16,8},{24,16},{9,1},{17,9},{25,17},{10,2},{18,10},{26,18},{... | collective-permute-start | bytes 36872 | tf_op jit(solution)/shard_map/ppermute | solution.py:256
  56.3 2.5 %collective-permute-start.6 = (f32[3,8,128]{2,1,0:T(8,128)S(1)}, f32[3,8,128]{2,1,0:T(8,128)S(1)}, u32[]{:S(2)}, u32[]{:S(2)}) collective-permute-start(f32[3,8,128]{2,1,0:T(8,128)S(1)} %get-tuple-element.6.own), channel_id=1, source_target_pairs={{0,8},{8,16},{16,24},{1,9},{9,17},{17,25},{2,10},{10,18},{18,26},{... | collective-permute-start | bytes 36872 | tf_op jit(solution)/shard_map/ppermute | solution.py:255
  60.0 0.0 collective-permute-done.7.after
  60.1 2.7 %collective-permute-done.6.before = f32[3,8,128]{2,1,0:T(8,128)S(1)} collective-permute-done((f32[3,8,128]{2,1,0:T(8,128)S(1)}, f32[3,8,128]{2,1,0:T(8,128)S(1)}, u32[]{:S(2)}, u32[]{:S(2)}) %collective-permute-start.6) | collective-permute-done | bytes 12320 | tf_op jit(solution)/shard_map/ppermute | solution.py:255
  62.8 0.0 all-to-all-done.proteins
  62.8 0.7 %shard_map.61 = (f32[3,8,128]{2,1,0:T(8,128)}, f32[1,1]{1,0:T(1,128)}) custom-call(s32[1]{0:T(128)S(6)} %copy.8.brackets, s32[1]{0:T(128)S(6)} %copy.9.codes, f32[3,8,128]{2,1,0:T(8,128)S(1)} %get-tuple-element.6.own, f32[3,8,128]{2,1,0:T(8,128)S(1)} %collective-permute-done.6.before, f32[3,8,128]{2,1,0:T(8,128)S(1)} %collective-permute-done.7.after, ...), custom_call_target="tpu_custom_call" | custom-call | tf_op jit(solution)/shard_map/pallas_call | solution.py:257
Async XLA Ops:
  0.6 9.9 %copy-start.2 = (s32[64,3]{0,1:T(4,128)S(1)}, s32[64,3]{0,1:T(4,128)}, u32[]{:S(2)}) copy-start(s32[64,3]{0,1:T(4,128)} %param.5) | copy-start | bytes 2308
  0.6 5.3 %collective-permute-start.3 = (f32[3,8,128]{2,1,0:T(8,128)}, f32[3,8,128]{2,1,0:T(8,128)S(1)}, u32[]{:S(2)}, u32[]{:S(2)}) collective-permute-start(f32[3,8,128]{2,1,0:T(8,128)} %bitcast.4), channel_id=1, source_target_pairs={{2,0},{3,1},{4,2},{5,3},{6,4},{7,5},{0,6},{1,7},{10,8},{11,9},{12,... | collective-permute-start | bytes 36872 | tf_op jit(solution)/shard_map/ppermute | solution.py:208
  4.3 1.7 %collective-permute-start.2 = (f32[3,8,128]{2,1,0:T(8,128)}, f32[3,8,128]{2,1,0:T(8,128)S(1)}, u32[]{:S(2)}, u32[]{:S(2)}) collective-permute-start(f32[3,8,128]{2,1,0:T(8,128)} %bitcast.5), channel_id=1, source_target_pairs={{1,0},{2,1},{3,2},{4,3},{5,4},{6,5},{7,6},{0,7},{9,8},{10,9},{11,1... | collective-permute-start | bytes 36872 | tf_op jit(solution)/shard_map/ppermute | solution.py:208
  4.3 5.1 %collective-permute-start.1 = (f32[3,8,128]{2,1,0:T(8,128)}, f32[3,8,128]{2,1,0:T(8,128)S(1)}, u32[]{:S(2)}, u32[]{:S(2)}) collective-permute-start(f32[3,8,128]{2,1,0:T(8,128)} %bitcast.6), channel_id=1, source_target_pairs={{7,0},{0,1},{1,2},{2,3},{3,4},{4,5},{5,6},{6,7},{15,8},{8,9},{9,10... | collective-permute-start | bytes 36872 | tf_op jit(solution)/shard_map/ppermute | solution.py:208
  4.8 5.7 %collective-permute-start = (f32[3,8,128]{2,1,0:T(8,128)}, f32[3,8,128]{2,1,0:T(8,128)S(1)}, u32[]{:S(2)}, u32[]{:S(2)}) collective-permute-start(f32[3,8,128]{2,1,0:T(8,128)} %bitcast.7), channel_id=1, source_target_pairs={{6,0},{7,1},{0,2},{1,3},{2,4},{3,5},{4,6},{5,7},{14,8},{15,9},{8,1... | collective-permute-start | bytes 36872 | tf_op jit(solution)/shard_map/ppermute | solution.py:208
  10.5 0.7 %copy-start = (f32[1,3,1024]{2,0,1:T(1,128)S(1)}, f32[1,3,1024]{2,0,1:T(1,128)}, u32[]{:S(2)}) copy-start(f32[1,3,1024]{2,0,1:T(1,128)} %param.4) | copy-start | bytes 36868
  11.2 26.1 %copy-start.1 = (f32[1,3,1024]{2,0,1:T(1,128)S(1)}, f32[1,3,1024]{2,0,1:T(1,128)}, u32[]{:S(2)}) copy-start(f32[1,3,1024]{2,0,1:T(1,128)} %param.4) | copy-start | bytes 36868
  32.2 1.5 %collective-permute-start.5 = (f32[3,8,128]{2,1,0:T(8,128)S(1)}, f32[3,8,128]{2,1,0:T(8,128)S(1)}, u32[]{:S(2)}, u32[]{:S(2)}) collective-permute-start(f32[3,8,128]{2,1,0:T(8,128)S(1)} %shard_map.59.refs_1_), channel_id=1, source_target_pairs={{1,0},{2,1},{3,2},{4,3},{5,4},{6,5},{7,6},{0,7},{9,8},{10,9},{11,1... | collective-permute-start | bytes 36872 | tf_op jit(solution)/shard_map/ppermute | solution.py:208
  32.4 4.9 %collective-permute-start.4 = (f32[3,8,128]{2,1,0:T(8,128)S(1)}, f32[3,8,128]{2,1,0:T(8,128)S(1)}, u32[]{:S(2)}, u32[]{:S(2)}) collective-permute-start(f32[3,8,128]{2,1,0:T(8,128)S(1)} %shard_map.59.refs_1_), channel_id=1, source_target_pairs={{7,0},{0,1},{1,2},{2,3},{3,4},{4,5},{5,6},{6,7},{15,8},{8,9},{9,10... | collective-permute-start | bytes 36872 | tf_op jit(solution)/shard_map/ppermute | solution.py:208
  49.9 12.9 %all-to-all-start = ((f32[32,3,128]{2,1,0:T(4,128)}), f32[32,3,128]{2,1,0:T(4,128)S(1)}, u32[]{:S(2)}, u32[]{:S(2)}) async-start(f32[32,3,128]{2,1,0:T(4,128)} %get-tuple-element.7), calls=%async_computation | async-start | bytes 131072 | tf_op jit(solution)/shard_map/all_to_all | solution.py:254
  52.9 7.2 %collective-permute-start.7 = (f32[3,8,128]{2,1,0:T(8,128)S(1)}, f32[3,8,128]{2,1,0:T(8,128)S(1)}, u32[]{:S(2)}, u32[]{:S(2)}) collective-permute-start(f32[3,8,128]{2,1,0:T(8,128)S(1)} %get-tuple-element.6.own), channel_id=1, source_target_pairs={{8,0},{16,8},{24,16},{9,1},{17,9},{25,17},{10,2},{18,10},{26,18},{... | collective-permute-start | bytes 36872 | tf_op jit(solution)/shard_map/ppermute | solution.py:256
  56.3 6.5 %collective-permute-start.6 = (f32[3,8,128]{2,1,0:T(8,128)S(1)}, f32[3,8,128]{2,1,0:T(8,128)S(1)}, u32[]{:S(2)}, u32[]{:S(2)}) collective-permute-start(f32[3,8,128]{2,1,0:T(8,128)S(1)} %get-tuple-element.6.own), channel_id=1, source_target_pairs={{0,8},{8,16},{16,24},{1,9},{9,17},{17,25},{2,10},{10,18},{18,26},{... | collective-permute-start | bytes 36872 | tf_op jit(solution)/shard_map/ppermute | solution.py:255

commit v3 on v2

--- a/solution.py
+++ b/solution.py
@@ -25,6 +25,8 @@
 SUB = 8
 GROUP = 4
 PAD = GROUP
+HALF = 8 * ROWS
+WIDTH = 2 * HALF
 PHASES = (6, 4)
 
 
@@ -39,31 +41,50 @@
     return lax.broadcasted_iota(jnp.int32, (ROWS, BLOCK), 0)
 
 
-def spread_matrix():
-    row = lax.broadcasted_iota(jnp.int32, (8 * ROWS, 3 * BLOCK), 0)
-    column = lax.broadcasted_iota(jnp.int32, (8 * ROWS, 3 * BLOCK), 1) // BLOCK
-    chosen = (row == column) | (row == column + 2 * ROWS) | (row == column + 5 * ROWS)
-    return jnp.where(chosen, 1.0, 0.0).astype(jnp.bfloat16)
-
-
-def place(u, block, refs, picks):
+def spread_matrices():
+    row = lax.broadcasted_iota(jnp.int32, (WIDTH, 2 * BLOCK), 0)
+    column = lax.broadcasted_iota(jnp.int32, (WIDTH, 2 * BLOCK), 1) // BLOCK
+
+    def picked(inner, component):
+        return (inner == component) | (inner == component + 2 * ROWS) | (inner == component + 5 * ROWS)
+
+    plane = picked(row, column)
+    depth = picked(row - HALF * column, 2)
+    return [jnp.where(chosen, 1.0, 0.0).astype(jnp.bfloat16) for chosen in (plane, depth)]
+
+
+def multiply(left, right):
+    return lax.dot_general(left, right, (((1,), (0,)), ((), ())), preferred_element_type=jnp.float32)
+
+
+def side_by_side(low, high):
+    lane = lax.broadcasted_iota(jnp.int32, (BLOCK, WIDTH), 1)
+    return jnp.where(lane < HALF, low, high)
+
+
+def place(new, base, refs, picks):
     state, left_feat, right_feat, columns = refs
     rows = row_ids()
-    u = jnp.where(rows < 3, u, 0.0)
-    norm = -0.5 * jnp.sum(u * u, axis=0, keepdims=True)
-    left = jnp.where(rows == 3, norm, jnp.where(rows == 4, 1.0, u))
-    right = jnp.where(rows == 4, norm, jnp.where(rows == 3, 1.0, u))
-    state[block] = u
-    l1, l2, l3 = parts_of(left)
-    r1, r2, r3 = parts_of(right)
-    zero = jnp.zeros_like(u)
-    stacked = jnp.concatenate([l1, l1, l2, l2, l1, l3, zero, zero], axis=0)
-    tall = stacked.T.astype(jnp.bfloat16)
-    left_feat[block] = tall
-    right_feat[block] = jnp.concatenate([r1, r2, r1, r2, r3, r1, zero, zero], axis=0).astype(jnp.bfloat16)
-    columns[block] = lax.dot_general(
-        tall, picks[...], (((1,), (0,)), ((), ())), preferred_element_type=jnp.float32
-    )
+    talls = []
+    for g, u in enumerate(new):
+        u = jnp.where(rows < 3, u, 0.0)
+        norm = -0.5 * jnp.sum(u * u, axis=0, keepdims=True)
+        left = jnp.where(rows == 3, norm, jnp.where(rows == 4, 1.0, u))
+        right = jnp.where(rows == 4, norm, jnp.where(rows == 3, 1.0, u))
+        state[base + g] = u
+        l1, l2, l3 = parts_of(left)
+        r1, r2, r3 = parts_of(right)
+        zero = jnp.zeros_like(u)
+        stacked = [l1, l1, l2, l2, l1, l3, zero, zero]
+        tall = jnp.concatenate(stacked + stacked, axis=0).T.astype(jnp.bfloat16)
+        left_feat[base + g] = tall
+        right_feat[base + g] = jnp.concatenate([r1, r2, r1, r2, r3, r1, zero, zero], axis=0).astype(jnp.bfloat16)
+        columns[base + g, :, : 2 * BLOCK] = multiply(tall, picks[0])
+        talls.append(tall)
+    for g in range(0, len(new), 2):
+        depth = multiply(side_by_side(talls[g], talls[g + 1]), picks[1])
+        columns[base + g, :, 2 * BLOCK :] = depth[:, :BLOCK]
+        columns[base + g + 1, :, 2 * BLOCK :] = depth[:, BLOCK:]
 
 
 def evolve_kernel(
@@ -75,14 +96,14 @@
         out, shared, refs = refs[0], refs[1], refs[2:]
     else:
         anchors, out, refs = slabs, refs[0], refs[1:]
-    first, picks, even, odd = refs[0], refs[1], refs[2:6], refs[6:]
+    first, picks, weights, even, odd = refs[0], refs[1], refs[2], refs[3:7], refs[7:]
     own_blocks = out.shape[1]
     partners = table.shape[0]
     total = table.shape[1]
     reach = HALO * steps
     blocks = own_blocks + 2 * reach
     slab = lax.axis_index("space")
-    picks[...] = spread_matrix()
+    picks[0], picks[1] = spread_matrices()
     filler = jnp.zeros((ROWS - 3, BLOCK), jnp.float32)
 
     def scaled(ref, block):
@@ -93,69 +114,107 @@
         begin, end = max(0, -shift), min(own_blocks, blocks - shift)
 
         def load(turn, carry, index=index, begin=begin, shift=shift):
+            block = begin + turn * GROUP
             for g in range(GROUP):
-                block = begin + turn * GROUP + g
-                first[block + shift + PAD] = scaled(anchors[index], block)
-                place(scaled(slabs[index], block), block + shift + PAD, even, picks)
+                first[block + g + shift + PAD] = scaled(anchors[index], block + g)
+            new = [scaled(slabs[index], block + g) for g in range(GROUP)]
+            place(new, block + shift + PAD, even, picks)
             return carry
 
         lax.fori_loop(0, (end - begin) // GROUP, load, 0)
 
-    def centre(block, source):
-        state, left_feat, right_feat, columns = source
-        spot = block - (PAD + reach)
-        row = lax.rem(slab * own_blocks + spot + total, total)
-        right = right_feat[block]
-        sums = [jnp.zeros((SUB, BLOCK), jnp.float32) for _ in range(4)]
-        for k in range(partners):
-            other = block + table[k, row] - HALO
-            power = lax.dot_general(
-                left_feat[other], right, (((1,), (0,)), ((), ())),
-                preferred_element_type=jnp.float32,
-            )
-            w = jnp.exp2(power)
-            for r in range(0, BLOCK, SUB):
-                piece = w[r : r + SUB]
-                sums[3] = sums[3] + piece
-                for c in range(3):
-                    sums[c] = sums[c] + piece * columns[other, pl.ds(r, SUB), c * BLOCK : (c + 1) * BLOCK]
+    def start_of(block):
+        return lax.rem(slab * own_blocks + (block - (PAD + reach)) + total, total)
+
+    def other_of(block, k):
+        return block + table[k, start_of(block)] - HALO
+
+    def powers(base, source):
+        _, left_feat, right_feat, _ = source
+        blank = jnp.zeros((HALF, BLOCK), jnp.bfloat16)
+        found = []
+        for block in [base + g for g in range(0, GROUP, 2)]:
+            right = jnp.concatenate([
+                jnp.concatenate([right_feat[block], blank], axis=1),
+                jnp.concatenate([blank, right_feat[block + 1]], axis=1),
+            ], axis=0)
+            found.append([
+                multiply(side_by_side(left_feat[other_of(block, k)], left_feat[other_of(block + 1, k)]), right)
+                for k in range(partners)
+            ])
+        return found
+
+    def keep_weights(found):
+        for p, row in enumerate(found):
+            for k, power in enumerate(row):
+                weights[p, k] = jnp.exp2(power)
+
+    def advance(base, source):
+        state, _, _, columns = source
         rows = row_ids()
-        sx, sy, sz, sw = [jnp.sum(s, axis=0, keepdims=True) for s in sums]
-        pulled = jnp.where(rows == 0, sx, jnp.where(rows == 1, sy, sz))
-        u = state[block]
-        force = (COUPLING / (partners * BLOCK)) * (u * sw - pulled)
-        inner = lax.rem(spot + own_blocks * near, own_blocks)
-        hold = jnp.where(inner * BLOCK < PROT_DEV, RESTRAINT, 0.0)
-        return u + TIME_STEP * (force - hold * (u - first[block]))
-
-    def step(turn, source, target, final=False):
-        low = HALO * (turn + 1) + PAD
-        groups = (blocks + 2 * PAD - 2 * low) // GROUP
-
-        def keep(new, base):
-            for g in range(GROUP):
-                if final:
-                    target[0][base + g] = new[g]
-                else:
-                    place(new[g], base + g, target, picks)
-
-        def group(index, held):
-            base = low + index * GROUP
-            keep(held, base - GROUP)
-            return tuple(centre(base + g, source) for g in range(GROUP))
-
-        start = tuple(jnp.zeros((ROWS, BLOCK), jnp.float32) for _ in range(GROUP))
-        held = lax.fori_loop(0, groups, group, start)
-        keep(held, low + (groups - 1) * GROUP)
-
-    def both(pair, carry):
-        step(2 * pair, even, odd)
-        step(2 * pair + 1, odd, even)
-        return carry
-
-    lax.fori_loop(0, steps // 2 - 1, both, 0)
-    step(steps - 2, even, odd)
-    step(steps - 1, odd, even, True)
+        found = []
+        for g in range(GROUP):
+            block = base + g
+            sums = [jnp.zeros((SUB, BLOCK), jnp.float32) for _ in range(4)]
+            lane = (g % 2) * BLOCK
+            for k in range(partners):
+                other = other_of(block, k)
+                for r in range(0, BLOCK, SUB):
+                    piece = weights[g // 2, k, r : r + SUB, lane : lane + BLOCK]
+                    sums[3] = sums[3] + piece
+                    for c in range(3):
+                        sums[c] = sums[c] + piece * columns[other, r : r + SUB, c * BLOCK : (c + 1) * BLOCK]
+            sx, sy, sz, sw = [jnp.sum(s, axis=0, keepdims=True) for s in sums]
+            pulled = jnp.where(rows == 0, sx, jnp.where(rows == 1, sy, sz))
+            u = state[block]
+            force = (COUPLING / (partners * BLOCK)) * (u * sw - pulled)
+            inner = lax.rem(block - (PAD + reach) + own_blocks * near, own_blocks)
+            hold = jnp.where(inner * BLOCK < PROT_DEV, RESTRAINT, 0.0)
+            found.append(u + TIME_STEP * (force - hold * (u - first[block])))
+        return tuple(found)
+
+    def turn(ask, move, store, held):
+        found = powers(*ask) if ask else None
+        new = advance(*move) if move else held
+        if ask:
+            keep_weights(found)
+        if store:
+            base, target = store
+            if target is None:
+                for g in range(GROUP):
+                    even[0][base + g] = held[g]
+            else:
+                place(held, base, target, picks)
+        return new
+
+    halves = (even, odd)
+    last = None
+    for t in range(steps):
+        source, target = halves[t % 2], halves[1 - t % 2] if t < steps - 1 else None
+        low = HALO * (t + 1) + PAD
+        count = (blocks + 2 * PAD - 2 * low) // GROUP
+
+        def at(g, refs, low=low):
+            return low + g * GROUP, refs
+
+        if t == 0:
+            turn(at(0, source), None, None, None)
+            held = turn(at(1, source), at(0, source), None, None)
+        elif last[0] < 4:
+            tail = turn(None, last[1](last[0] - 1, last[2]), last[1](last[0] - 2, last[3]), held)
+            turn(at(0, source), None, last[1](last[0] - 1, last[3]), tail)
+            held = turn(at(1, source), at(0, source), None, None)
+        else:
+            held = turn(at(0, source), last[1](last[0] - 1, last[2]), last[1](last[0] - 2, last[3]), held)
+            held = turn(at(1, source), at(0, source), last[1](last[0] - 1, last[3]), held)
+
+        def steady(g, held, at=at, source=source, target=target):
+            return turn(at(g, source), at(g - 1, source), at(g - 2, target), held)
+
+        held = lax.fori_loop(2, count, steady, held)
+        last = (count, at, source, target)
+    tail = turn(None, last[1](last[0] - 1, last[2]), last[1](last[0] - 2, None), held)
+    turn(None, None, last[1](last[0] - 1, None), tail)
     for a in range(own_blocks):
         out[:, a, :] = even[0][PAD + reach + a, :3] * (1.0 / SCALE)
     if copies:
@@ -218,8 +277,8 @@
         outs.append(jax.ShapeDtypeStruct((copies, 3, PROT_DEV), jnp.float32))
     half = [
         pltpu.VMEM((blocks, ROWS, BLOCK), jnp.float32),
-        pltpu.VMEM((blocks, BLOCK, 8 * ROWS), jnp.bfloat16),
-        pltpu.VMEM((blocks, 8 * ROWS, BLOCK), jnp.bfloat16),
+        pltpu.VMEM((blocks, BLOCK, WIDTH), jnp.bfloat16),
+        pltpu.VMEM((blocks, HALF, BLOCK), jnp.bfloat16),
         pltpu.VMEM((blocks, BLOCK, 3 * BLOCK), jnp.float32),
     ]
     return pl.pallas_call(
@@ -229,7 +288,8 @@
         out_specs=[VMEM] * len(outs),
         scratch_shapes=[
             pltpu.VMEM((blocks, ROWS, BLOCK), jnp.float32),
-            pltpu.VMEM((8 * ROWS, 3 * BLOCK), jnp.bfloat16),
+            pltpu.VMEM((2, WIDTH, 2 * BLOCK), jnp.bfloat16),
+            pltpu.VMEM((GROUP // 2, table.shape[0], BLOCK, 2 * BLOCK), jnp.float32),
             *half,
             *half,
         ],

time: 63.8 us -> 54.4 us (0.85)
  Pallas kernels: 34.3 us -> 24.7 us
    pallas_call x2, Pallas kernels: 33.6 us -> 24 us  [evolve(): pl.pallas_call(functools.partial(evolve_kernel, steps, near, copies), out...]
where the time goes in v3:
time: 54.4 us; the launch traced here: 54.1 us
  Pallas kernels  24.7 us (45%)
  starting transfers between devices  14.3 us (26%)
  waiting for transfers between devices  12.4 us (23%)
  between operations  1.97 us (4%)
  local copies, waits for them, and re-layouts  0.72 us (1%)
    pallas_call x2, Pallas kernels, evolve(): pl.pallas_call(functools.partial(evolve_kernel, steps, near, copies), out...  24 us
    ppermute x6, waiting for transfers between devices, around(): found.append(lax.ppermute(cells, 'space', route) if distance else cells)  9.68 us
    ppermute x6, starting transfers between devices, around(): found.append(lax.ppermute(cells, 'space', route) if distance else cells)  5.4 us
    ppermute x1, starting transfers between devices, body(): after = lax.ppermute(evolved, 'image', down)  3.37 us
    all_to_all x1, starting transfers between devices, body(): proteins = lax.all_to_all(shared, ('image', 'space'), 0, 0, tiled=True)  3.06 us
    ppermute x1, waiting for transfers between devices, body(): before = lax.ppermute(evolved, 'image', up)  2.71 us
    ppermute x1, starting transfers between devices, body(): before = lax.ppermute(evolved, 'image', up)  2.47 us
  transfers between devices with their start and end apart: 9, of which 7 were waited for; matrix products, arithmetic and copies ran while one was open for 0% of the time, Pallas kernels for 0%

profile of v3, /device:TPU:4, one launch (start us, length us, event | category | flops | bytes accessed | tf_op | source)
XLA Modules:
  0.0 54.1 jit_solution(16313637593755597839)
XLA Ops:
  0.6 0.0 copy-start.2
  0.6 3.7 %collective-permute-start.3 = (f32[3,8,128]{2,1,0:T(8,128)}, f32[3,8,128]{2,1,0:T(8,128)S(1)}, u32[]{:S(2)}, u32[]{:S(2)}) collective-permute-start(f32[3,8,128]{2,1,0:T(8,128)} %bitcast.4), channel_id=1, source_target_pairs={{2,0},{3,1},{4,2},{5,3},{6,4},{7,5},{0,6},{1,7},{10,8},{11,9},{12,... | collective-permute-start | bytes 36872 | tf_op jit(solution)/shard_map/ppermute | solution.py:267
  4.3 0.0 collective-permute-start.2
  4.3 0.5 collective-permute-start.1
  4.8 0.7 %collective-permute-start = (f32[3,8,128]{2,1,0:T(8,128)}, f32[3,8,128]{2,1,0:T(8,128)S(1)}, u32[]{:S(2)}, u32[]{:S(2)}) collective-permute-start(f32[3,8,128]{2,1,0:T(8,128)} %bitcast.7), channel_id=1, source_target_pairs={{6,0},{7,1},{0,2},{1,3},{2,4},{3,5},{4,6},{5,7},{14,8},{15,9},{8,1... | collective-permute-start | bytes 36872 | tf_op jit(solution)/shard_map/ppermute | solution.py:267
  5.5 0.4 collective-permute-done.3.refs_4_
  5.9 0.1 collective-permute-done.2.refs_3_.refs_5_
  6.0 3.4 %collective-permute-done.1.refs_1_.refs_3_ = f32[3,8,128]{2,1,0:T(8,128)S(1)} collective-permute-done((f32[3,8,128]{2,1,0:T(8,128)}, f32[3,8,128]{2,1,0:T(8,128)S(1)}, u32[]{:S(2)}, u32[]{:S(2)}) %collective-permute-start.1) | collective-permute-done | bytes 12320 | tf_op jit(solution)/shard_map/ppermute | solution.py:267
  9.4 1.1 %collective-permute-done.refs_0_ = f32[3,8,128]{2,1,0:T(8,128)S(1)} collective-permute-done((f32[3,8,128]{2,1,0:T(8,128)}, f32[3,8,128]{2,1,0:T(8,128)S(1)}, u32[]{:S(2)}, u32[]{:S(2)}) %collective-permute-start) | collective-permute-done | bytes 12320 | tf_op jit(solution)/shard_map/ppermute | solution.py:267
  10.5 0.0 copy-done.2
  10.5 0.0 copy-start
  10.5 0.7 %copy-done = f32[1,3,1024]{2,0,1:T(1,128)S(1)} copy-done((f32[1,3,1024]{2,0,1:T(1,128)S(1)}, f32[1,3,1024]{2,0,1:T(1,128)}, u32[]{:S(2)}) %copy-start) | copy-done | bytes 12312
  11.2 0.0 copy-start.1
  11.2 14.7 %shard_map.59.refs_1_ = f32[3,8,128]{2,1,0:T(8,128)S(1)} custom-call(s32[3,64]{1,0:T(4,128)S(1)} %bitcast.10, f32[3,8,128]{2,1,0:T(8,128)S(1)} %collective-permute-done.refs_0_, f32[3,8,128]{2,1,0:T(8,128)S(1)} %collective-permute-done.1.refs_1_.refs_3_, f32[3,8,128]{2,1,0:T(8,128)S(1)} %bitcast.8, f32[3,8,128]{2,1,0:T(8,128)S(1)} %collective-permute-done.2.refs_3_.refs_5_, ...), custom_call_target="tpu_custom_call" | custom-call | tf_op jit(solution)/shard_map/pallas_call | solution.py:284
  25.9 0.1 collective-permute-start.5
  26.1 0.4 collective-permute-start.4
  26.5 1.0 %collective-permute-done.5.refs_2_ = f32[3,8,128]{2,1,0:T(8,128)S(1)} collective-permute-done((f32[3,8,128]{2,1,0:T(8,128)S(1)}, f32[3,8,128]{2,1,0:T(8,128)S(1)}, u32[]{:S(2)}, u32[]{:S(2)}) %collective-permute-start.5) | collective-permute-done | bytes 12320 | tf_op jit(solution)/shard_map/ppermute | solution.py:267
  27.5 3.7 %collective-permute-done.4.refs_0_ = f32[3,8,128]{2,1,0:T(8,128)S(1)} collective-permute-done((f32[3,8,128]{2,1,0:T(8,128)S(1)}, f32[3,8,128]{2,1,0:T(8,128)S(1)}, u32[]{:S(2)}, u32[]{:S(2)}) %collective-permute-start.4) | collective-permute-done | bytes 12320 | tf_op jit(solution)/shard_map/ppermute | solution.py:267
  31.1 0.0 copy-done.1
  31.1 9.3 %shard_map.60 = (f32[3,8,128]{2,1,0:T(8,128)S(1)}, f32[32,3,128]{2,1,0:T(4,128)}) custom-call(s32[3,64]{1,0:T(4,128)S(1)} %bitcast.11, f32[3,8,128]{2,1,0:T(8,128)S(1)} %collective-permute-done.4.refs_0_, f32[3,8,128]{2,1,0:T(8,128)S(1)} %shard_map.59.refs_1_, f32[3,8,128]{2,1,0:T(8,128)S(1)} %collective-permute-done.5.refs_2_, ...), custom_call_target="tpu_custom_call" | custom-call | tf_op jit(solution)/shard_map/pallas_call | solution.py:284
  40.4 3.1 %all-to-all-start = ((f32[32,3,128]{2,1,0:T(4,128)}), f32[32,3,128]{2,1,0:T(4,128)S(1)}, u32[]{:S(2)}, u32[]{:S(2)}) async-start(f32[32,3,128]{2,1,0:T(4,128)} %get-tuple-element.7), calls=%async_computation | async-start | bytes 131072 | tf_op jit(solution)/shard_map/all_to_all | solution.py:314
  43.5 3.4 %collective-permute-start.7 = (f32[3,8,128]{2,1,0:T(8,128)S(1)}, f32[3,8,128]{2,1,0:T(8,128)S(1)}, u32[]{:S(2)}, u32[]{:S(2)}) collective-permute-start(f32[3,8,128]{2,1,0:T(8,128)S(1)} %get-tuple-element.6.own), channel_id=1, source_target_pairs={{8,0},{16,8},{24,16},{9,1},{17,9},{25,17},{10,2},{18,10},{26,18},{... | collective-permute-start | bytes 36872 | tf_op jit(solution)/shard_map/ppermute | solution.py:316
  46.9 2.5 %collective-permute-start.6 = (f32[3,8,128]{2,1,0:T(8,128)S(1)}, f32[3,8,128]{2,1,0:T(8,128)S(1)}, u32[]{:S(2)}, u32[]{:S(2)}) collective-permute-start(f32[3,8,128]{2,1,0:T(8,128)S(1)} %get-tuple-element.6.own), channel_id=1, source_target_pairs={{0,8},{8,16},{16,24},{1,9},{9,17},{17,25},{2,10},{10,18},{18,26},{... | collective-permute-start | bytes 36872 | tf_op jit(solution)/shard_map/ppermute | solution.py:315
  50.6 0.0 collective-permute-done.7.after
  50.6 2.7 %collective-permute-done.6.before = f32[3,8,128]{2,1,0:T(8,128)S(1)} collective-permute-done((f32[3,8,128]{2,1,0:T(8,128)S(1)}, f32[3,8,128]{2,1,0:T(8,128)S(1)}, u32[]{:S(2)}, u32[]{:S(2)}) %collective-permute-start.6) | collective-permute-done | bytes 12320 | tf_op jit(solution)/shard_map/ppermute | solution.py:315
  53.3 0.0 all-to-all-done.proteins
  53.3 0.7 %shard_map.61 = (f32[3,8,128]{2,1,0:T(8,128)}, f32[1,1]{1,0:T(1,128)}) custom-call(s32[1]{0:T(128)S(6)} %copy.8.brackets, s32[1]{0:T(128)S(6)} %copy.9.codes, f32[3,8,128]{2,1,0:T(8,128)S(1)} %get-tuple-element.6.own, f32[3,8,128]{2,1,0:T(8,128)S(1)} %collective-permute-done.6.before, f32[3,8,128]{2,1,0:T(8,128)S(1)} %collective-permute-done.7.after, ...), custom_call_target="tpu_custom_call" | custom-call | tf_op jit(solution)/shard_map/pallas_call | solution.py:317
Async XLA Ops:
  0.6 9.9 %copy-start.2 = (s32[64,3]{0,1:T(4,128)S(1)}, s32[64,3]{0,1:T(4,128)}, u32[]{:S(2)}) copy-start(s32[64,3]{0,1:T(4,128)} %param.5) | copy-start | bytes 2308
  0.6 5.3 %collective-permute-start.3 = (f32[3,8,128]{2,1,0:T(8,128)}, f32[3,8,128]{2,1,0:T(8,128)S(1)}, u32[]{:S(2)}, u32[]{:S(2)}) collective-permute-start(f32[3,8,128]{2,1,0:T(8,128)} %bitcast.4), channel_id=1, source_target_pairs={{2,0},{3,1},{4,2},{5,3},{6,4},{7,5},{0,6},{1,7},{10,8},{11,9},{12,... | collective-permute-start | bytes 36872 | tf_op jit(solution)/shard_map/ppermute | solution.py:267
  4.3 1.7 %collective-permute-start.2 = (f32[3,8,128]{2,1,0:T(8,128)}, f32[3,8,128]{2,1,0:T(8,128)S(1)}, u32[]{:S(2)}, u32[]{:S(2)}) collective-permute-start(f32[3,8,128]{2,1,0:T(8,128)} %bitcast.5), channel_id=1, source_target_pairs={{1,0},{2,1},{3,2},{4,3},{5,4},{6,5},{7,6},{0,7},{9,8},{10,9},{11,1... | collective-permute-start | bytes 36872 | tf_op jit(solution)/shard_map/ppermute | solution.py:267
  4.3 5.1 %collective-permute-start.1 = (f32[3,8,128]{2,1,0:T(8,128)}, f32[3,8,128]{2,1,0:T(8,128)S(1)}, u32[]{:S(2)}, u32[]{:S(2)}) collective-permute-start(f32[3,8,128]{2,1,0:T(8,128)} %bitcast.6), channel_id=1, source_target_pairs={{7,0},{0,1},{1,2},{2,3},{3,4},{4,5},{5,6},{6,7},{15,8},{8,9},{9,10... | collective-permute-start | bytes 36872 | tf_op jit(solution)/shard_map/ppermute | solution.py:267
  4.8 5.7 %collective-permute-start = (f32[3,8,128]{2,1,0:T(8,128)}, f32[3,8,128]{2,1,0:T(8,128)S(1)}, u32[]{:S(2)}, u32[]{:S(2)}) collective-permute-start(f32[3,8,128]{2,1,0:T(8,128)} %bitcast.7), channel_id=1, source_target_pairs={{6,0},{7,1},{0,2},{1,3},{2,4},{3,5},{4,6},{5,7},{14,8},{15,9},{8,1... | collective-permute-start | bytes 36872 | tf_op jit(solution)/shard_map/ppermute | solution.py:267
  10.5 0.7 %copy-start = (f32[1,3,1024]{2,0,1:T(1,128)S(1)}, f32[1,3,1024]{2,0,1:T(1,128)}, u32[]{:S(2)}) copy-start(f32[1,3,1024]{2,0,1:T(1,128)} %param.4) | copy-start | bytes 36868
  11.2 19.9 %copy-start.1 = (f32[1,3,1024]{2,0,1:T(1,128)S(1)}, f32[1,3,1024]{2,0,1:T(1,128)}, u32[]{:S(2)}) copy-start(f32[1,3,1024]{2,0,1:T(1,128)} %param.4) | copy-start | bytes 36868
  25.9 1.5 %collective-permute-start.5 = (f32[3,8,128]{2,1,0:T(8,128)S(1)}, f32[3,8,128]{2,1,0:T(8,128)S(1)}, u32[]{:S(2)}, u32[]{:S(2)}) collective-permute-start(f32[3,8,128]{2,1,0:T(8,128)S(1)} %shard_map.59.refs_1_), channel_id=1, source_target_pairs={{1,0},{2,1},{3,2},{4,3},{5,4},{6,5},{7,6},{0,7},{9,8},{10,9},{11,1... | collective-permute-start | bytes 36872 | tf_op jit(solution)/shard_map/ppermute | solution.py:267
  26.1 5.1 %collective-permute-start.4 = (f32[3,8,128]{2,1,0:T(8,128)S(1)}, f32[3,8,128]{2,1,0:T(8,128)S(1)}, u32[]{:S(2)}, u32[]{:S(2)}) collective-permute-start(f32[3,8,128]{2,1,0:T(8,128)S(1)} %shard_map.59.refs_1_), channel_id=1, source_target_pairs={{7,0},{0,1},{1,2},{2,3},{3,4},{4,5},{5,6},{6,7},{15,8},{8,9},{9,10... | collective-permute-start | bytes 36872 | tf_op jit(solution)/shard_map/ppermute | solution.py:267
  40.4 12.9 %all-to-all-start = ((f32[32,3,128]{2,1,0:T(4,128)}), f32[32,3,128]{2,1,0:T(4,128)S(1)}, u32[]{:S(2)}, u32[]{:S(2)}) async-start(f32[32,3,128]{2,1,0:T(4,128)} %get-tuple-element.7), calls=%async_computation | async-start | bytes 131072 | tf_op jit(solution)/shard_map/all_to_all | solution.py:314
  43.5 7.2 %collective-permute-start.7 = (f32[3,8,128]{2,1,0:T(8,128)S(1)}, f32[3,8,128]{2,1,0:T(8,128)S(1)}, u32[]{:S(2)}, u32[]{:S(2)}) collective-permute-start(f32[3,8,128]{2,1,0:T(8,128)S(1)} %get-tuple-element.6.own), channel_id=1, source_target_pairs={{8,0},{16,8},{24,16},{9,1},{17,9},{25,17},{10,2},{18,10},{26,18},{... | collective-permute-start | bytes 36872 | tf_op jit(solution)/shard_map/ppermute | solution.py:316
  46.9 6.5 %collective-permute-start.6 = (f32[3,8,128]{2,1,0:T(8,128)S(1)}, f32[3,8,128]{2,1,0:T(8,128)S(1)}, u32[]{:S(2)}, u32[]{:S(2)}) collective-permute-start(f32[3,8,128]{2,1,0:T(8,128)S(1)} %get-tuple-element.6.own), channel_id=1, source_target_pairs={{0,8},{8,16},{16,24},{1,9},{9,17},{17,25},{2,10},{10,18},{18,26},{... | collective-permute-start | bytes 36872 | tf_op jit(solution)/shard_map/ppermute | solution.py:315
